TPU v7x, 32 devices: a whole 2x2x4 slice. The times are simulated.
32 devices in a mesh: row: 4 (over y, x), col: 8 (over z, core).
Axes of the slice: x: 2, y: 2, z: 4, core: 2. Of those that a mesh axis runs over, the one named last changes fastest.
Arguments:
- known_inverse: float32 [12288, 12288], P('col', 'row'), may hold values from -6 to 6
- factor_sep: float32 [12288, 1536], P('col'), may hold values from -0.09375 to 0.09375
- factor_pair: float32 [1536, 1536], P('col'), may hold values from -0.25 to 0.25
- pivot_inverse: float32 [1536, 1536], P('col', 'row'), may hold values from -6 to 6
- widths: int32 [8], replicated, may hold values from 1 to 512, 1536 in all
- parent_of: int32 [8], replicated, may hold values from -1 to 7, as said below
- ancestors: int32 [8, 24], replicated, may hold values from 0 to 63, all different within a row
Outputs:
- panel_inverse: float32 [1536, 12288], P('col', 'row')
- block_inverse: float32 [1536, 1536], P('col', 'row')
Inputs may be any that keep to these rules, and one draw needn't show every extreme that they name: `parent_of`: exactly 4 supernodes have -1; each other one names one of those. `ancestors`: each supernode lists different blocks; every block is listed by some supernode. The widths sum to 1536.
All inputs are finite; a program needn't handle non-finite values.
Results may differ from a plain program's by a relative error of at most 0.0003.
Values sent between devices are 32-bit elements; how exact they have to be, the bound alone decides.
A program may use at most 192 MiB of HBM per device.

v0:
```python
import jax
import jax.numpy as jnp
from jax import lax
from jax.sharding import PartitionSpec as P

NS = 12288
WTOT = 1536
NSUP = 8
NBLK = 64


exact_mode = lax.Precision.HIGH
panel_chunks = 4


def plain_dot(left, right):
    return jnp.dot(left, right, precision=exact_mode, preferred_element_type=jnp.float32)


def first_dot(left, right):
    return lax.dot_general(
        left,
        right,
        (((0,), (0,)), ((), ())),
        precision=exact_mode,
        preferred_element_type=jnp.float32,
    )


def supernode_tables(widths, parent_of, ancestors):
    position = jnp.arange(WTOT, dtype=jnp.int32)
    width_ends = jnp.cumsum(widths)
    column_owner = jnp.sum((width_ends[None, :] <= position[:, None]).astype(jnp.int32), axis=1)
    owner_onehot = column_owner[:, None] == jnp.arange(NSUP, dtype=jnp.int32)[None, :]
    listed = jnp.any(
        ancestors[:, :, None] == jnp.arange(NBLK, dtype=jnp.int32)[None, None, :], axis=1
    ).astype(jnp.float32)
    column_blocks = plain_dot(owner_onehot.astype(jnp.float32), listed)
    column_parent = jnp.sum(jnp.where(owner_onehot, parent_of[None, :], 0), axis=1)
    column_upper = column_parent < 0
    return (column_owner, column_blocks, column_parent, column_upper)


def shards(known_inverse, factor_sep, factor_pair, pivot_inverse, widths, parent_of, ancestors):
    col_index = lax.axis_index("col")
    row_index = lax.axis_index("row")
    rows = lax.axis_size("row")
    cols = lax.axis_size("col")
    fold_ratio = cols // rows
    sep_local = factor_sep.shape[0]
    pair_local = factor_pair.shape[0]
    wide_local = pivot_inverse.shape[1]
    column_owner, column_blocks, column_parent, column_upper = supernode_tables(
        widths, parent_of, ancestors
    )
    sep_index = col_index * sep_local + jnp.arange(sep_local, dtype=jnp.int32)
    block_onehot = (
        (sep_index // (NS // NBLK))[:, None] == jnp.arange(NBLK, dtype=jnp.int32)[None, :]
    ).astype(jnp.float32)
    sep_factor = factor_sep * plain_dot(block_onehot, column_blocks.T)
    upper_cols = column_upper.astype(jnp.float32)
    lower_cols = 1.0 - upper_cols
    owner_rows = lax.dynamic_slice_in_dim(column_owner, col_index * pair_local, pair_local)
    owner_wide = lax.dynamic_slice_in_dim(column_owner, row_index * wide_local, wide_local)
    parent_wide = lax.dynamic_slice_in_dim(column_parent, row_index * wide_local, wide_local)
    upper_rows = lax.dynamic_slice_in_dim(upper_cols, col_index * pair_local, pair_local)
    upper_wide = lax.dynamic_slice_in_dim(column_upper, row_index * wide_local, wide_local)
    coupling = jnp.where(
        (owner_rows[:, None] == column_parent[None, :]) & (~column_upper)[None, :], factor_pair, 0.0
    )
    matching = owner_rows[:, None] == owner_wide[None, :]
    match_lower = matching & (~upper_wide)[None, :]
    match_pair = owner_rows[:, None] == parent_wide[None, :]
    match_upper_all = (owner_rows[:, None] == column_owner[None, :]) & column_upper[None, :]

    coupling_all = lax.all_gather(coupling, "col", axis=0, tiled=True)

    piece_rows = sep_local // rows
    piece = lax.dynamic_slice_in_dim(sep_factor, row_index * piece_rows, piece_rows)
    deal = [
        (r * cols + c, (c // fold_ratio) * cols + (c % fold_ratio) * rows + r)
        for r in range(rows)
        for c in range(cols)
    ]
    piece = lax.ppermute(piece, ("row", "col"), deal)
    piece, coupling_all = lax.optimization_barrier((piece, coupling_all))
    sep_cols = lax.all_gather(piece, "col", axis=0, tiled=True)

    lead = plain_dot(sep_factor * upper_cols[None, :], coupling_all) - sep_factor
    step = known_inverse.shape[1] // panel_chunks
    panels = []
    product = jnp.zeros((pair_local, WTOT), jnp.float32)
    for i in range(panel_chunks):
        part = first_dot(lead, known_inverse[:, i * step : (i + 1) * step])
        panels.append(lax.psum_scatter(part, "col", scatter_dimension=0, tiled=True))
    for i in range(panel_chunks):
        product = product + plain_dot(panels[i], sep_cols[i * step : (i + 1) * step])
    panel = jnp.concatenate(panels, 1)

    own_pivot = lax.dynamic_update_slice_in_dim(
        jnp.zeros_like(product), jnp.where(matching, pivot_inverse, 0.0), row_index * wide_local, 1
    )
    deficit = lax.psum(product - own_pivot, "row")
    upper_block_all = jnp.where(match_upper_all, -deficit, 0.0)
    pair_rows = -(
        deficit * upper_rows[:, None] * lower_cols[None, :]
        + plain_dot(upper_block_all, coupling_all)
    )
    pair_cols = lax.all_to_all(pair_rows, "col", split_axis=1, concat_axis=0, tiled=True)
    coupling_own = lax.dynamic_slice_in_dim(coupling_all, row_index * wide_local, wide_local, 1)

    def own_cols(x):
        return lax.dynamic_slice_in_dim(x, row_index * wide_local, wide_local, 1)

    pair_block = jnp.where(match_pair, own_cols(pair_rows), 0.0)
    lower_block = jnp.where(
        match_lower, -own_cols(deficit) - first_dot(pair_cols, coupling_own), 0.0
    )
    return (panel, own_cols(upper_block_all) + lower_block + pair_block)


def solution(mesh):
    in_specs = (P("col", "row"), P("col", None), P("col", None), P("col", "row"), P(), P(), P())
    out_specs = (P("col", "row"), P("col", "row"))
    return jax.shard_map(shards, mesh=mesh, in_specs=in_specs, out_specs=out_specs, check_vma=False)
```

profile of v0, /device:TPU:0, one launch (start us, length us, event | category | flops | bytes accessed | tf_op | source)
XLA Modules:
  0.0 751.8 jit_solution(14991458933092573735)
XLA Ops:
  7.2 0.8 reduce-window.8
  8.0 0.1 convert_reduce_fusion
  8.1 0.7 select_reduce_fusion
  8.9 0.1 dynamic_slice.31
  9.0 0.6 broadcast_subtract_fusion
  9.6 2.6 and_select_fusion
  12.3 0.8 fusion.51
  13.1 0.3 fusion.52
  13.3 5.8 convolution_multiply_fusion
  19.1 3.8 copy-done
  22.9 0.2 constant_dynamic-slice_fusion
  23.1 0.8 collective-permute-start
  23.9 147.2 %all-gather.3.cloned.1.call-done = f32[1536,1536]{1,0:T(8,128)} async-done(((f32[192,1536]{1,0:T(8,128)}), f32[1536,1536]{1,0:T(8,128)}) %all-gather.3.cloned.1.call-update) | async-done | bytes 9437200 | tf_op jit(solution)/shard_map/all_gather | solution.py:76
  171.1 29.8 %fusion.2 = f32[1536,1536]{1,0:T(8,128)S(1)} fusion(f32[1536,1536]{1,0:T(8,128)} %copy-done, f32[1536,1536]{1,0:T(8,128)} %all-gather.3.cloned.1.call-done, f32[1536]{0:T(1024)S(1)} %get-tuple-element.8), kind=kOutput, calls=%fused_computation.3 | convolution fusion | flops 21747990528 | bytes 28317696 | tf_op jit(solution)/shard_map/dot_general | solution.py:17
  201.0 3.7 copy-done.14
  204.6 26.7 %fusion.15 = f32[1536,768]{1,0:T(8,128)} fusion(f32[1536,1536]{1,0:T(8,128)S(1)} %fusion.2, f32[1536,3072]{1,0:T(8,128)} %param.7), kind=kOutput, calls=%fused_computation.14 | convolution fusion | flops 10871635968 | bytes 18874368 | tf_op jit(solution)/shard_map/dot_general | solution.py:21
  231.4 0.7 all-gather.5.cloned.1.call-update
  232.1 17.8 %fusion.17 = f32[1536,768]{1,0:T(8,128)} fusion(f32[1536,1536]{1,0:T(8,128)} %copy-done.14, f32[1536,3072]{1,0:T(8,128)} %param.7), kind=kOutput, calls=%fused_computation.16 | convolution fusion | flops 10871635968 | bytes 18874368 | tf_op jit(solution)/shard_map/dot_general | solution.py:21
  250.0 0.0 reduce-scatter.5.cloned.1.call-start
  250.0 17.6 %fusion.19 = f32[1536,768]{1,0:T(8,128)} fusion(f32[1536,1536]{1,0:T(8,128)} %copy-done.14, f32[1536,3072]{1,0:T(8,128)} %param.7), kind=kOutput, calls=%fused_computation.18 | convolution fusion | flops 10871635968 | bytes 18874368 | tf_op jit(solution)/shard_map/dot_general | solution.py:21
  267.7 0.0 reduce-scatter.11.cloned.1.call-start
  267.7 17.7 %fusion.13 = f32[1536,768]{1,0:T(8,128)} fusion(f32[1536,1536]{1,0:T(8,128)} %copy-done.14, f32[1536,3072]{1,0:T(8,128)} %param.7), kind=kOutput, calls=%fused_computation.12 | convolution fusion | flops 10871635968 | bytes 18874368 | tf_op jit(solution)/shard_map/dot_general | solution.py:21
  285.4 0.3 all-reduce.2.cloned.1.call-start
  285.7 0.1 dynamic_slice.32
  285.8 1.2 broadcast_in_dim.24
  286.9 0.8 fusion.50
  287.8 5.4 reduce-scatter.9.cloned.1.call-done
  293.1 169.0 %all-gather.5.cloned.1.call-done = f32[3072,1536]{1,0:T(8,128)} async-done(((f32[384,1536]{1,0:T(8,128)}), f32[3072,1536]{1,0:T(8,128)}) %all-gather.5.cloned.1.call-update) | async-done | bytes 18874384 | tf_op jit(solution)/shard_map/all_gather | solution.py:87
  462.1 4.3 fusion.7
  466.4 50.9 %reduce-scatter.7.cloned.1.call-done = f32[192,768]{1,0:T(8,128)} async-done(((f32[1536,768]{1,0:T(8,128)}), f32[192,768]{1,0:T(8,128)}) %reduce-scatter.7.cloned.1.call-update) | async-done | bytes 589840 | tf_op jit(solution)/shard_map/reduce_scatter | solution.py:95
  517.4 4.3 fusion.9
  521.7 51.2 %reduce-scatter.5.cloned.1.call-done = f32[192,768]{1,0:T(8,128)} async-done(((f32[1536,768]{1,0:T(8,128)}), f32[192,768]{1,0:T(8,128)}) %reduce-scatter.5.cloned.1.call-update) | async-done | bytes 589840 | tf_op jit(solution)/shard_map/reduce_scatter | solution.py:95
  572.9 4.3 fusion.31
  577.3 51.2 %reduce-scatter.11.cloned.1.call-done = f32[192,768]{1,0:T(8,128)} async-done(((f32[1536,768]{1,0:T(8,128)}), f32[192,768]{1,0:T(8,128)}) %reduce-scatter.11.cloned.1.call-update) | async-done | bytes 589840 | tf_op jit(solution)/shard_map/reduce_scatter | solution.py:95
  628.4 5.7 fusion.28
  634.2 0.8 dynamic_slice.36
  634.9 52.2 %all-reduce.2.cloned.1.call-done = f32[192,1536]{1,0:T(8,128)} async-done(((f32[192,1536]{1,0:T(8,128)}), f32[192,1536]{1,0:T(8,128)}) %all-reduce.2.cloned.1.call-update) | async-done | bytes 1179664 | tf_op jit(solution)/shard_map/psum | solution.py:103
  687.1 7.8 %fusion.34 = f32[192,1536]{1,0:T(8,128)S(1)} fusion(f32[1536,1536]{1,0:T(8,128)} %all-gather.3.cloned.1.call-done, f32[192,1536]{1,0:T(8,128)} %all-reduce.2.cloned.1.call-done, f32[1536]{0:T(1024)S(1)} %copy-done.8, f32[192]{0:T(256)S(1)} %dynamic_slice.36, s32[1536]{0:T(1024)S(1)} %convert_reduce_fusion, s32[192]{0:T(256)S(1)} %copy-done.7, ...), kind=kOutput, calls=%fused_computation.26 | convolution fusion | flops 2720268288 | bytes 11811840 | tf_op jit(solution)/shard_map/dot_general | solution.py:17
  695.0 1.6 copy.14
  696.6 4.9 all-to-all-start
  701.5 0.1 dynamic_slice.38
  701.6 0.1 dynamic-slice_not_fusion
  701.7 3.1 pad_maximum_fusion
  704.8 1.3 negate_select_fusion
  706.1 33.2 %all-to-all-done = f32[192,8,192]{0,2,1:T(8,128)S(1)} async-done(((f32[192,8,192]{0,2,1:T(8,128)}), f32[192,8,192]{0,2,1:T(8,128)S(1)}, u32[]{:S(2)}, u32[]{:S(2)}) %all-to-all-start) | async-done | bytes 1179680 | tf_op jit(solution)/shard_map/all_to_all | solution.py:109
  739.3 0.9 copy.13
  740.2 0.5 all_to_all.17
  740.8 3.8 fusion.46
  (41 shorter events, 0.3 us)
Async XLA Ops:
  7.2 164.0 %all-gather.3.cloned.1.call-start = ((), (), s32[]{:S(2)}) async-start(), calls=%async_computation.5 | async-start | bytes 10616832 | tf_op jit(solution)/shard_map/all_gather | solution.py:76
  9.0 278.0 %copy-start.6 = (s32[192]{0:T(256)}, s32[192]{0:T(256)S(1)}, u32[]{:S(2)}) copy-start(s32[192]{0:T(256)S(1)} %dynamic_slice.31) | copy-start | bytes 2308
  9.6 2.7 copy-start.9
  9.6 161.5 %copy-start.13 = (f32[1536]{0:T(1024)}, f32[1536]{0:T(1024)S(1)}, u32[]{:S(2)}) copy-start(f32[1536]{0:T(1024)S(1)} %get-tuple-element.8) | copy-start | bytes 18436
  12.2 280.9 %reduce-scatter.9.cloned.1.call-start = ((), (), s32[]{:S(2)}) async-start(), calls=%async_computation.8 | async-start | bytes 5308416 | tf_op jit(solution)/shard_map/reduce_scatter | solution.py:95
  19.1 3.8 copy-start
  23.1 0.8 collective-permute-start
  23.9 177.0 %copy-start.4 = (f32[384,1536]{1,0:T(8,128)}, f32[384,1536]{1,0:T(8,128)S(1)}, u32[]{:S(2)}) copy-start(f32[384,1536]{1,0:T(8,128)S(1)} %collective-permute-done) | copy-start | bytes 7077892
  200.9 3.7 copy-start.14
  231.3 230.8 %all-gather.5.cloned.1.call-start = ((), (), s32[]{:S(2)}) async-start(), calls=%async_computation.10 | async-start | bytes 21233664 | tf_op jit(solution)/shard_map/all_gather | solution.py:87
  232.1 285.3 %reduce-scatter.7.cloned.1.call-start = ((), (), s32[]{:S(2)}) async-start(), calls=%async_computation.7 | async-start | bytes 5308416 | tf_op jit(solution)/shard_map/reduce_scatter | solution.py:95
  250.0 323.0 %reduce-scatter.5.cloned.1.call-start = ((), (), s32[]{:S(2)}) async-start(), calls=%async_computation.6 | async-start | bytes 5308416 | tf_op jit(solution)/shard_map/reduce_scatter | solution.py:95
  267.7 360.8 %reduce-scatter.11.cloned.1.call-start = ((), (), s32[]{:S(2)}) async-start(), calls=%async_computation.9 | async-start | bytes 5308416 | tf_op jit(solution)/shard_map/reduce_scatter | solution.py:95
  285.4 1.6 copy-start.5
  285.4 401.7 %all-reduce.2.cloned.1.call-start = ((), (), s32[]{:S(2)}) async-start(), calls=%async_computation.11 | async-start | bytes 2359296 | tf_op jit(solution)/shard_map/psum | solution.py:103
  285.8 180.7 %copy-start.11 = (s32[384]{0:T(512)}, s32[384]{0:T(512)S(1)}, u32[]{:S(2)}) copy-start(s32[384]{0:T(512)S(1)} %dynamic_slice.32) | copy-start | bytes 4612
  577.3 109.9 %copy-start.7 = (s32[192]{0:T(256)S(1)}, s32[192]{0:T(256)}, u32[]{:S(2)}) copy-start(s32[192]{0:T(256)} %copy-done.6) | copy-start | bytes 2308
  577.3 109.9 %copy-start.8 = (f32[1536]{0:T(1024)S(1)}, f32[1536]{0:T(1024)}, u32[]{:S(2)}) copy-start(f32[1536]{0:T(1024)} %get-tuple-element.6) | copy-start | bytes 18436
  577.3 109.9 %copy-start.10 = (pred[1536]{0:T(1024)(128)(4,1)S(1)}, pred[1536]{0:T(1024)(128)(4,1)}, u32[]{:S(2)}) copy-start(pred[1536]{0:T(1024)(128)(4,1)} %copy-done.9) | copy-start | bytes 4612
  695.0 1.7 copy-start.2
  695.0 6.7 copy-start.3
  695.0 9.8 %copy-start.1 = (f32[192,1536]{1,0:T(8,128)S(1)}, f32[192,1536]{1,0:T(8,128)}, u32[]{:S(2)}) copy-start(f32[192,1536]{1,0:T(8,128)} %all-reduce.2.cloned.1.call-done) | copy-start | bytes 3538948
  696.6 42.6 %all-to-all-start = ((f32[192,8,192]{0,2,1:T(8,128)}), f32[192,8,192]{0,2,1:T(8,128)S(1)}, u32[]{:S(2)}, u32[]{:S(2)}) async-start(f32[192,8,192]{0,2,1:T(8,128)} %bitcast.2), calls=%async_computation.4 | async-start | bytes 3145728 | tf_op jit(solution)/shard_map/all_to_all | solution.py:109
  704.8 36.0 %copy-start.12 = (s32[384]{0:T(512)S(1)}, s32[384]{0:T(512)}, u32[]{:S(2)}) copy-start(s32[384]{0:T(512)} %copy-done.11) | copy-start | bytes 4612
Sparse Core Ops, SparseCore 0:
  12.3 158.7 all-gather.2
  231.4 61.6 reduce-scatter.8
  295.3 166.7 all-gather.4
  464.3 53.0 reduce-scatter.6
  519.5 53.3 reduce-scatter.4
  575.1 53.3 reduce-scatter.10
  634.3 52.8 all-reduce.1
where the time goes:
time: 759 us; the launch traced here: 752 us
  waiting for transfers between devices  561 us (74%)
  matrix products  146 us (19%)
  between operations  14.8 us (2%)
  local copies, waits for them, and re-layouts  12.9 us (2%)
  other arithmetic  10.9 us (1%)
    all_gather x1, waiting for transfers between devices, shards(): sep_cols = lax.all_gather(piece, 'col', axis=0, tiled=True)  169 us
    reduce_scatter x4, waiting for transfers between devices, shards(): lax.psum_scatter(part, 'col', scatter_dimension=0, tiled=True)  159 us
    all_gather x1, waiting for transfers between devices, shards(): coupling_all = lax.all_gather(coupling, 'col', axis=0, tiled=True)  147 us
    dot_general x5, matrix products, first_dot(): lax.dot_general(left, right, (((0,), (0,)), ((), ())), precision=exact_mo...  83.6 us
    dot_general x8, matrix products, plain_dot(): jnp.dot(left, right, precision=exact_mode, preferred_element_type=jnp.flo...  62.3 us
    psum x1, waiting for transfers between devices, shards(): deficit = lax.psum(product - own_pivot, 'row')  52.2 us
    all_to_all x1, waiting for transfers between devices, shards(): lax.all_to_all(pair_rows, 'col', split_axis=1, concat_axis=0, tiled=True)  33.2 us
  transfers between devices with their start and end apart: 9, of which 8 were waited for; matrix products, arithmetic and copies ran while one was open for 11% of the time, Pallas kernels for 0%

commit v1 on v0

v1 whole, which is shorter than its diff:
```python
import functools

import jax
import jax.numpy as jnp
from jax import lax
from jax.experimental import pallas as pl
from jax.experimental.pallas import tpu as pltpu
from jax.sharding import PartitionSpec as P

NS = 12288
WTOT = 1536
NSUP = 8
NBLK = 64

MESH = pl.DeviceIdType.MESH
exact_mode = lax.Precision.HIGH


def plain_dot(left, right):
    return jnp.dot(left, right, precision=exact_mode, preferred_element_type=jnp.float32)


def first_dot(left, right):
    return lax.dot_general(
        left,
        right,
        (((0,), (0,)), ((), ())),
        precision=exact_mode,
        preferred_element_type=jnp.float32,
    )

def supernode_tables(widths, parent_of, ancestors):
    position = jnp.arange(WTOT, dtype=jnp.int32)
    width_ends = jnp.cumsum(widths)
    column_owner = jnp.sum((width_ends[None, :] <= position[:, None]).astype(jnp.int32), axis=1)
    owner_onehot = column_owner[:, None] == jnp.arange(NSUP, dtype=jnp.int32)[None, :]
    listed = jnp.any(
        ancestors[:, :, None] == jnp.arange(NBLK, dtype=jnp.int32)[None, None, :], axis=1
    ).astype(jnp.float32)
    column_blocks = plain_dot(owner_onehot.astype(jnp.float32), listed)
    column_parent = jnp.sum(jnp.where(owner_onehot, parent_of[None, :], 0), axis=1)
    column_upper = column_parent < 0
    return (column_owner, column_blocks, column_parent, column_upper)


def line_kernel(chunks, chips, width, deal, *refs):
    if deal:
        high, low, known, panel, dealt, own, pair, below, above, sems, *refs = refs
        deal_send, deal_recv, fetched, known_high, known_low, sent, fetch = refs
    else:
        part, panel, own, pair, below, above, sems = refs
    load, pair_send, pair_recv, up_send, up_recv, down_send, down_recv, store = (
        sems.at[i] for i in range(8)
    )
    row = lax.axis_index("row")
    col = lax.axis_index("col")
    chip = col // 2
    core = col % 2
    other = col + 1 - 2 * core
    last = chips - 1
    half = max(chunks // 2, 1)
    lag = 2 if deal else 0
    depth = panel.shape[0]

    barrier = pltpu.get_barrier_semaphore()

    def greet(device):
        pl.semaphore_signal(barrier, inc=1, device_id=device, device_id_type=MESH)

    greet((row, other))

    @pl.when(chip > 0)
    def _():
        greet((row, col - 2))

    @pl.when(chip < last)
    def _():
        greet((row, col + 2))

    met = 1 + (chip > 0).astype(jnp.int32) + (chip < last).astype(jnp.int32)
    if deal:

        @pl.when(chip != row)
        def _():
            greet((chip, 2 * row))
            greet((chip, 2 * row + 1))

        met = met + 2 * (chip != row).astype(jnp.int32)
    pl.semaphore_wait(barrier, met)

    def span(j):
        if chunks == 1:
            return pl.ds(0, width)
        return pl.ds(pl.multiple_of(j * width, width), width)

    def load_copy(j):
        return pltpu.make_async_copy(part.at[:, core, :, span(j)], own.at[j], load.at[j])

    def remote(src, dst, send, recv, device):
        return pltpu.make_async_remote_copy(
            src_ref=src, dst_ref=dst, send_sem=send, recv_sem=recv,
            device_id=device, device_id_type=MESH,
        )

    def pair_copy(j):
        source = sent.at[j % 4] if deal else part.at[:, 1 - core, :, span(j)]
        return remote(source, pair.at[j], pair_send.at[j], pair_recv.at[j], (row, other))

    def fetch_copy(g):
        columns = pl.ds(pl.multiple_of(2 * g * width, 2 * width), 2 * width)
        return pltpu.make_async_copy(known.at[:, columns], fetched.at[g % 2], fetch.at[g % 2])

    def up_copy(j, at):
        units = pl.ds(at + 1, last - at)
        return remote(own.at[j, units], below.at[j, units], up_send.at[j], up_recv.at[j], (row, col + 2))

    def down_copy(j, at):
        units = pl.ds(0, at)
        return remote(own.at[j, units], above.at[j, units], down_send.at[j], down_recv.at[j], (row, col - 2))

    def store_copy(j):
        return pltpu.make_async_copy(own.at[j, chip], panel.at[:, span(j)], store.at[j])

    def kept(j):
        return (chip == row) & (j // half == core)

    def deal_spot(j):
        return dealt.at[core, :, span(j % half)]

    def deal_copy(j):
        return remote(
            own.at[j, chip], deal_spot(j), deal_send.at[j], deal_recv.at[core, j % half],
            (chip, 2 * row + j // half),
        )

    def keep_copy(j):
        return pltpu.make_async_copy(own.at[j, chip], deal_spot(j), deal_recv.at[core, j % half])

    def begin(j, carry):
        load_copy(j).start()
        pair_copy(j).start()
        return carry

    if deal:
        fetch_copy(0).start()
    else:
        lax.fori_loop(0, chunks, begin, 0)

    def multiply(t):
        g = t // 2
        fetch_copy(g).wait()

        @pl.when(g + 1 < half)
        def _():
            fetch_copy(g + 1).start()

        @pl.when(t >= 4)
        def _():
            pair_copy(t - 4).wait_send()
            pair_copy(t - 3).wait_send()

        def split(i, carry):
            at = pl.ds(pl.multiple_of(i * 2 * width, 2 * width), 2 * width)
            block = fetched[g % 2, at, :]
            rounded = block.astype(jnp.bfloat16)
            known_high[at, :] = rounded
            known_low[at, :] = (block - rounded.astype(jnp.float32)).astype(jnp.bfloat16)
            return carry

        lax.fori_loop(0, fetched.shape[1] // (2 * width), split, 0)

        def unit(d, carry):
            at = pl.ds(pl.multiple_of(d * 2 * depth, 2 * depth), 2 * depth)
            total = jnp.dot(high[at, :], known_low[...], preferred_element_type=jnp.float32)
            total += jnp.dot(low[at, :], known_high[...], preferred_element_type=jnp.float32)
            total += jnp.dot(high[at, :], known_high[...], preferred_element_type=jnp.float32)
            for side in range(2):

                @pl.when(core == side)
                def _():
                    for i in range(2):
                        piece = total[:, i * width : (i + 1) * width]
                        own[t + i, d] = piece[side * depth : (side + 1) * depth]
                        sent[(t + i) % 4, d] = piece[(1 - side) * depth : (2 - side) * depth]

            return carry

        lax.fori_loop(0, chips, unit, 0)

    def tick(t, carry):
        if deal:

            @pl.when((t < chunks) & (t % 2 == 0))
            def _():
                multiply(t)

        sum_at = t - lag

        @pl.when((sum_at >= 0) & (sum_at < chunks))
        def _():
            if not deal:
                load_copy(sum_at).wait()
            pair_copy(sum_at).wait_recv()
            own[sum_at] = own[sum_at] + pair[sum_at]

        if deal:

            @pl.when((t < chunks) & (t % 2 == 0))
            def _():
                pair_copy(t).start()
                pair_copy(t + 1).start()

        up = sum_at - chip
        down = sum_at - (last - chip)
        ready = sum_at - jnp.maximum(chip, last - chip)
        for at in range(chips):

            @pl.when((chip == at) & (up >= 0) & (up < chunks))
            def _():
                if at > 0:
                    up_copy(up, at - 1).wait_recv()
                    for d in range(at, chips):
                        own[up, d] = own[up, d] + below[up, d]

            @pl.when((chip == at) & (down >= 0) & (down < chunks))
            def _():
                if at < last:
                    down_copy(down, at + 1).wait_recv()
                    for d in range(at + 1):
                        own[down, d] = own[down, d] + above[down, d]

            @pl.when((chip == at) & (up >= 0) & (up < chunks))
            def _():
                if at < last:
                    up_copy(up, at).start()

            @pl.when((chip == at) & (down >= 0) & (down < chunks))
            def _():
                if at > 0:
                    down_copy(down, at).start()

        @pl.when((ready >= 0) & (ready < chunks))
        def _():
            store_copy(ready).start()
            if deal:

                @pl.when(kept(ready))
                def _():
                    keep_copy(ready).start()

                @pl.when(jnp.logical_not(kept(ready)))
                def _():
                    deal_copy(ready).start()

        return carry

    lax.fori_loop(0, chunks + last + lag, tick, 0)

    def finish(j, carry):
        @pl.when(j >= (chunks - 4 if deal else 0))
        def _():
            pair_copy(j).wait_send()

        store_copy(j).wait()
        for at in range(chips):

            @pl.when(chip == at)
            def _():
                if at < last:
                    up_copy(j, at).wait_send()
                if at > 0:
                    down_copy(j, at).wait_send()

        if deal:

            @pl.when(jnp.logical_not(kept(j)))
            def _():
                deal_copy(j).wait_send()

        return carry

    lax.fori_loop(0, chunks, finish, 0)
    if deal:

        def landed(i, carry):
            spot = dealt.at[i // half, :, span(i % half)]
            pltpu.make_async_copy(own.at[0, 0], spot, deal_recv.at[i // half, i % half]).wait()
            return carry

        lax.fori_loop(0, 2 * half, landed, 0)


ANYWHERE = pl.BlockSpec(memory_space=pl.ANY)


def line_params(number):
    return pltpu.CompilerParams(
        collective_id=number, has_side_effects=True, vmem_limit_bytes=62 << 20
    )


def line_scratch(chunks, chips, depth, width):
    block = pltpu.VMEM((chunks, chips, depth, width), jnp.float32)
    return [block] * 4 + [pltpu.SemaphoreType.DMA((8, chunks))]


def panel_reduce(high, low, known, chips, depth):
    inner, wide = known.shape
    width = 128
    chunks = wide // width
    return pl.pallas_call(
        functools.partial(line_kernel, chunks, chips, width, True),
        out_shape=[
            jax.ShapeDtypeStruct((depth, wide), jnp.float32),
            jax.ShapeDtypeStruct((2, depth, wide // 2), jnp.float32),
        ],
        in_specs=[pl.BlockSpec(memory_space=pltpu.VMEM)] * 2 + [ANYWHERE],
        out_specs=[ANYWHERE] * 2,
        scratch_shapes=line_scratch(chunks, chips, depth, width)
        + [
            pltpu.SemaphoreType.DMA((chunks,)),
            pltpu.SemaphoreType.DMA((2, chunks // 2)),
            pltpu.VMEM((2, inner, 2 * width), jnp.float32),
            pltpu.VMEM((inner, 2 * width), jnp.bfloat16),
            pltpu.VMEM((inner, 2 * width), jnp.bfloat16),
            pltpu.VMEM((4, chips, depth, width), jnp.float32),
            pltpu.SemaphoreType.DMA((2,)),
        ],
        compiler_params=line_params(1),
        name="panel_reduce",
    )(high, low, known)


def block_reduce(part):
    chips, _, depth, wide = part.shape
    chunks = wide // 128 if wide % 128 == 0 else 1
    return pl.pallas_call(
        functools.partial(line_kernel, chunks, chips, wide // chunks, False),
        out_shape=jax.ShapeDtypeStruct((depth, wide), jnp.float32),
        in_specs=[ANYWHERE],
        out_specs=ANYWHERE,
        scratch_shapes=line_scratch(chunks, chips, depth, wide // chunks),
        compiler_params=line_params(2),
        name="block_reduce",
    )(part)


def plane_kernel(rows, part, total, arrived, sends, recvs):
    row = lax.axis_index("row")
    col = lax.axis_index("col")
    tall = total.shape[1]
    barrier = pltpu.get_barrier_semaphore()
    for step in range(1, rows):
        device = (lax.rem(row + step, rows), col)
        pl.semaphore_signal(barrier, inc=1, device_id=device, device_id_type=MESH)
    pl.semaphore_wait(barrier, rows - 1)

    def copy(step):
        target = lax.rem(row + step, rows)
        columns = pl.ds(pl.multiple_of(target * tall, tall), tall)
        return pltpu.make_async_remote_copy(
            src_ref=part.at[:, columns], dst_ref=arrived.at[step],
            send_sem=sends.at[step], recv_sem=recvs.at[step],
            device_id=(target, col), device_id_type=MESH,
        )

    for step in range(1, rows):
        copy(step).start()
    columns = pl.ds(pl.multiple_of(row * tall, tall), tall)
    mine = pltpu.make_async_copy(part.at[:, columns], arrived.at[0], recvs.at[0])
    mine.start()
    mine.wait()
    for step in range(1, rows):
        copy(step).wait()
    result = arrived[0]
    for step in range(1, rows):
        result = result + arrived[step]
    total[...] = result


def plane_reduce(part, rows):
    depth, wide = part.shape
    tall = wide // rows
    if tall % 128:
        return lax.psum_scatter(part, "row", scatter_dimension=1, tiled=True)
    return pl.pallas_call(
        functools.partial(plane_kernel, rows),
        out_shape=jax.ShapeDtypeStruct((depth, tall), jnp.float32),
        in_specs=[ANYWHERE],
        out_specs=pl.BlockSpec(memory_space=pltpu.VMEM),
        scratch_shapes=[
            pltpu.VMEM((rows, depth, tall), jnp.float32),
            pltpu.SemaphoreType.DMA((rows,)),
            pltpu.SemaphoreType.DMA((rows,)),
        ],
        compiler_params=line_params(3),
        name="plane_reduce",
    )(part)


def gather_kernel(chips, mine, out, held, sems, stores):
    row = lax.axis_index("row")
    col = lax.axis_index("col")
    chip = col // 2
    core = col % 2
    other = col + 1 - 2 * core
    last = chips - 1
    piece = held.shape[2]
    along_x, along_y, across = row + 1 - 2 * (row % 2), (row + 2) % 4, 3 - row

    barrier = pltpu.get_barrier_semaphore()

    def greet(device):
        pl.semaphore_signal(barrier, inc=1, device_id=device, device_id_type=MESH)

    greet((row, other))
    greet((along_x, col))
    greet((along_y, col))

    @pl.when(chip > 0)
    def _():
        greet((row, col - 2))

    @pl.when(chip < last)
    def _():
        greet((row, col + 2))

    met = 3 + (chip > 0).astype(jnp.int32) + (chip < last).astype(jnp.int32)
    pl.semaphore_wait(barrier, met)

    def remote(ref, send, recv, spot, device):
        return pltpu.make_async_remote_copy(
            src_ref=ref, dst_ref=ref, send_sem=sems.at[send, spot], recv_sem=sems.at[recv, spot],
            device_id=device, device_id_type=MESH,
        )

    def item(at, quarter):
        return held.at[2 * at + core, quarter]

    def up(at):
        return remote(item(at, row), 0, 2, at, (row, col + 2))

    def down(at):
        return remote(item(at, row), 1, 2, at, (row, col - 2))

    def sideways_x(at):
        return remote(item(at, row), 3, 4, at, (along_x, col))

    def sideways_y(at):
        return remote(item(at, row), 5, 6, at, (along_y, col))

    def onward_x(at):
        return remote(item(at, along_y).at[pl.ds(0, piece // 2)], 7, 8, at, (along_x, col))

    def onward_y(at):
        return remote(
            item(at, along_x).at[pl.ds(piece // 2, piece // 2)], 9, 10, at, (along_y, col)
        )

    def hand(at, quarter):
        return remote(item(at, quarter), 11 + quarter, 15 + quarter, at, (row, other))

    def hand_own():
        return remote(held.at[col], 19, 20, 0, (row, other))

    def keep(c):
        return pltpu.make_async_copy(held.at[c], out.at[c], stores.at[c])

    def both_ways(visit):
        for distance in range(1, chips):

            @pl.when(chip - distance >= 0)
            def _():
                visit(chip - distance, True)

            @pl.when(chip + distance <= last)
            def _():
                visit(chip + distance, False)

    load = pltpu.make_async_copy(mine, held.at[col], sems.at[21, 0])
    load.start()
    load.wait()

    @pl.when(chip < last)
    def _():
        up(chip).start()

    @pl.when(chip > 0)
    def _():
        down(chip).start()

    hand_own().start()
    keep(col).start()

    def from_line(at, rising):
        if rising:
            up(at).wait_recv()

            @pl.when(chip < last)
            def _():
                up(at).start()

        else:
            down(at).wait_recv()

            @pl.when(chip > 0)
            def _():
                down(at).start()

        sideways_x(at).start()
        sideways_y(at).start()
        hand(at, row).start()

    def from_sides(at, rising):
        sideways_x(at).wait_recv()
        onward_y(at).start()
        hand(at, along_x).start()
        sideways_y(at).wait_recv()
        onward_x(at).start()
        hand(at, along_y).start()

    def from_across(at, rising):
        onward_x(at).wait_recv()
        onward_y(at).wait_recv()
        hand(at, across).start()
        keep(2 * at + core).start()

    def from_other(at, rising):
        for quarter in range(4):
            hand(at, quarter).wait_recv()
        keep(2 * at + 1 - core).start()

    both_ways(from_line)
    both_ways(from_sides)
    both_ways(from_across)
    hand_own().wait_recv()
    keep(other).start()
    both_ways(from_other)

    def drain(at, rising):
        if rising:

            @pl.when(chip < last)
            def _():
                up(at).wait_send()

        else:

            @pl.when(chip > 0)
            def _():
                down(at).wait_send()

        for copy in (sideways_x, sideways_y, onward_x, onward_y):
            copy(at).wait_send()
        for quarter in range(4):
            hand(at, quarter).wait_send()

    both_ways(drain)

    @pl.when(chip < last)
    def _():
        up(chip).wait_send()

    @pl.when(chip > 0)
    def _():
        down(chip).wait_send()

    hand_own().wait_send()
    for c in range(2 * chips):
        keep(c).wait()


def gather_rows(mine, rows, cols):
    depth, wide = mine.shape
    piece = depth // 4
    if rows != 4 or piece % 16:
        return lax.all_gather(mine, "col", axis=0, tiled=True)
    shape = (cols, 4, piece, wide)
    out = pl.pallas_call(
        functools.partial(gather_kernel, cols // 2),
        out_shape=jax.ShapeDtypeStruct(shape, jnp.float32),
        in_specs=[ANYWHERE],
        out_specs=ANYWHERE,
        scratch_shapes=[
            pltpu.VMEM(shape, jnp.float32),
            pltpu.SemaphoreType.DMA((22, cols // 2)),
            pltpu.SemaphoreType.DMA((cols,)),
        ],
        compiler_params=line_params(4),
        name="gather_rows",
    )(mine.reshape(4, piece, wide))
    return out.reshape(cols * depth, wide)


def shards(known_inverse, factor_sep, factor_pair, pivot_inverse, widths, parent_of, ancestors):
    col_index = lax.axis_index("col")
    row_index = lax.axis_index("row")
    rows = lax.axis_size("row")
    cols = lax.axis_size("col")
    chips = cols // 2
    chip, core = col_index // 2, col_index % 2
    sep_local = factor_sep.shape[0]
    pair_local = factor_pair.shape[0]
    wide_local = pivot_inverse.shape[1]
    column_owner, column_blocks, column_parent, column_upper = supernode_tables(
        widths, parent_of, ancestors
    )

    def rows_of(x, index, size):
        return lax.dynamic_slice_in_dim(x, index * size, size)

    def cols_of(x, index, size):
        return lax.dynamic_slice_in_dim(x, index * size, size, 1)

    sep_index = col_index * sep_local + jnp.arange(sep_local, dtype=jnp.int32)
    block_onehot = (
        (sep_index // (NS // NBLK))[:, None] == jnp.arange(NBLK, dtype=jnp.int32)[None, :]
    ).astype(jnp.float32)
    sep_factor = factor_sep * plain_dot(block_onehot, column_blocks.T)
    upper_cols = column_upper.astype(jnp.float32)
    owner_rows = rows_of(column_owner, col_index, pair_local)
    owner_wide = rows_of(column_owner, row_index, wide_local)
    parent_wide = rows_of(column_parent, row_index, wide_local)
    upper_wide = rows_of(column_upper, row_index, wide_local)
    coupling = jnp.where(
        (owner_rows[:, None] == column_parent[None, :]) & (~column_upper)[None, :], factor_pair, 0.0
    )
    matching = owner_rows[:, None] == owner_wide[None, :]
    match_pair = owner_rows[:, None] == parent_wide[None, :]

    coupling_all = gather_rows(coupling, rows, cols)

    straight = [
        (r * cols + 2 * z + q, z * cols + 2 * r + q)
        for r in range(rows)
        for z in range(chips)
        for q in range(2)
    ]
    crossed = [(source, target ^ 1) for source, target in straight]
    swapped = [(device, device ^ 1) for device in range(rows * cols)]

    def permute(x, order):
        return lax.ppermute(x, ("row", "col"), order)

    def ordered(mine, others):
        return jnp.where(
            core == 0, jnp.concatenate([mine, others]), jnp.concatenate([others, mine])
        )

    upper_pivot = jnp.where(matching & upper_wide[None, :], pivot_inverse, 0.0)
    pivot_tile = ordered(
        permute(cols_of(upper_pivot, core, pair_local), straight),
        permute(cols_of(upper_pivot, 1 - core, pair_local), crossed),
    )
    pivot_coupled = plain_dot(pivot_tile, coupling)

    lead = plain_dot(sep_factor * upper_cols[None, :], coupling_all) - sep_factor
    turned = lead.T
    high = lax.reduce_precision(turned, 8, 7)
    low = (turned - high).astype(jnp.bfloat16)
    panel, dealt = panel_reduce(
        high.astype(jnp.bfloat16), low, known_inverse, chips, pair_local
    )
    moved = dealt.reshape(wide_local, sep_local)

    moved_upper = jnp.where(upper_wide[:, None], moved, 0.0)
    moved_lower = jnp.where(upper_wide[:, None], 0.0, moved)
    product = plain_dot(moved_lower, sep_factor) - plain_dot(moved_upper, lead) + pivot_coupled
    product = product.reshape(2, pair_local, chips, wide_local).transpose(2, 0, 1, 3)
    tile = block_reduce(product)

    dealt_tile = permute(tile, straight)
    pair_tile = jnp.where(
        rows_of(column_owner, 2 * row_index + core, pair_local)[:, None]
        == rows_of(column_parent, chip, wide_local)[None, :],
        -tile,
        0.0,
    )
    pair_cols = ordered(
        cols_of(pair_tile, core, pair_local),
        permute(cols_of(pair_tile, 1 - core, pair_local), swapped),
    )
    below = first_dot(pair_cols, rows_of(coupling_all, row_index, wide_local))
    below = plane_reduce(below, rows)

    own_block = jnp.where(
        matching, pivot_inverse - dealt_tile - jnp.where(upper_wide[None, :], 0.0, below), 0.0
    )
    return panel, own_block + jnp.where(match_pair, -dealt_tile, 0.0)


def solution(mesh):
    if mesh.shape["col"] != 2 * mesh.shape["row"]:
        raise ValueError("unsupported mesh")
    in_specs = (P("col", "row"), P("col", None), P("col", None), P("col", "row"), P(), P(), P())
    out_specs = (P("col", "row"), P("col", "row"))
    return jax.shard_map(shards, mesh=mesh, in_specs=in_specs, out_specs=out_specs, check_vma=False)
```

time: 759 us -> 458 us (0.60)
  waiting for transfers between devices: 561 us -> 1.44 us
  Pallas kernels: 0 us -> 359 us
  matrix products: 146 us -> 60.9 us
  between operations: 14.8 us -> 0.91 us
    pallas_call x0 -> x4, Pallas kernels: none -> 359 us  [the longest x1 239 us: panel_reduce(): pl.pallas_call(functools.partial(line_kernel, chunks, chips, width, True)...]
    all_gather x2 -> x0, waiting for transfers between devices: 316 us -> none  [the longest x1 169 us: shards(): sep_cols = lax.all_gather(piece, 'col', axis=0, tiled=True)]
    reduce_scatter x4 -> x0, waiting for transfers between devices: 159 us -> none  [shards(): lax.psum_scatter(part, 'col', scatter_dimension=0, tiled=True)]
    dot_general x5 -> x1, matrix products: 83.6 us -> 3.9 us  [first_dot(): lax.dot_general(left, right, (((0,), (0,)), ((), ())), precision=exact_mo...]
    psum x1 -> x0, waiting for transfers between devices: 52.2 us -> none  [shards(): deficit = lax.psum(product - own_pivot, 'row')]
    all_to_all x1 -> x0, waiting for transfers between devices: 33.2 us -> none  [shards(): lax.all_to_all(pair_rows, 'col', split_axis=1, concat_axis=0, tiled=True)]
    dot_general x8 -> x6, matrix products: 62.3 us -> 57 us  [plain_dot(): jnp.dot(left, right, precision=exact_mode, preferred_element_type=jnp.flo...]
  transfers between devices with their start and end apart: 9 -> 4, of which waited for: 8 -> 1; matrix products, arithmetic and copies ran while one was open for 11% -> 16% of each run, Pallas kernels for 0% -> 71%
where the time goes in v1:
time: 458 us
  Pallas kernels  359 us (78%)
  matrix products  60.9 us (13%)
  local copies, waits for them, and re-layouts  19.7 us (4%)
  other arithmetic  10.5 us (2%)
  starting transfers between devices  5.17 us (1%)
    pallas_call x1, Pallas kernels, panel_reduce(): pl.pallas_call(functools.partial(line_kernel, chunks, chips, width, True)...  239 us
    pallas_call x1, Pallas kernels, gather_rows(): pl.pallas_call(functools.partial(gather_kernel, cols // 2), out_shape=jax...  61.6 us
    dot_general x6, matrix products, plain_dot(): jnp.dot(left, right, precision=exact_mode, preferred_element_type=jnp.flo...  57 us
    pallas_call x1, Pallas kernels, block_reduce(): pl.pallas_call(functools.partial(line_kernel, chunks, chips, wide // chun...  34.3 us
    pallas_call x1, Pallas kernels, plane_reduce(): pl.pallas_call(functools.partial(plane_kernel, rows), out_shape=jax.Shape...  24.3 us
    unnamed x22, local copies, waits for them, and re-layouts  12.9 us
  transfers between devices with their start and end apart: 4, of which 1 were waited for; matrix products, arithmetic and copies ran while one was open for 16% of the time, Pallas kernels for 71%

profile of v1, /device:TPU:0, one launch (start us, length us, event | category | flops | bytes accessed | tf_op | source)
XLA Modules:
  0.0 457.6 jit_solution(10975770221246382114)
XLA Ops:
  0.7 0.8 reduce-window.8
  1.5 0.1 convert_reduce_fusion
  1.6 0.7 select_reduce_fusion
  2.3 0.1 dynamic_slice.34
  2.4 0.1 dynamic_slice.35
  2.5 0.6 fusion.33
  3.1 1.1 fusion.21
  4.2 0.9 constant_dynamic-slice_fusion.3
  5.1 3.0 collective-permute-start
  8.1 0.5 collective-permute-start.1
  8.6 2.5 and_select_fusion
  11.2 61.6 %gather_rows.1 = f32[8,4,48,1536]{3,2,1,0:T(8,128)} custom-call(f32[4,48,1536]{2,1,0:T(8,128)} %bitcast.23), custom_call_target="tpu_custom_call" | custom-call | tf_op jit(solution)/shard_map/gather_rows/pallas_call | solution.py:579
  72.8 0.0 copy-done.9
  72.8 0.1 fusion.24
  72.9 0.3 fusion.25
  73.2 9.6 %copy.16 = f32[1536,1536]{0,1:T(8,128)} copy(f32[1536,1536]{1,0:T(8,128)} %param.8) | data formatting | bytes 18874368 | tf_op args[1]
  82.7 5.9 %convolution_multiply_fusion = f32[1536,1536]{0,1:T(8,128)S(1)} fusion(f32[1536,1536]{0,1:T(8,128)} %copy.16, f32[1536,64]{0,1:T(8,128)S(1)} %fusion.25, s32[1536]{0:T(1024)S(1)} %add_select_fusion), kind=kOutput, calls=%fused_computation.2 | convolution fusion | flops 908427264 | bytes 19273728 | tf_op jit(solution)/shard_map/dot_general | solution.py:20
  88.7 0.0 copy-start
  88.7 31.9 %fusion = (bf16[1536,1536]{1,0:T(8,128)(2,1)}, bf16[1536,1536]{1,0:T(8,128)(2,1)}, f32[1536,1536]{0,1:T(8,128)}) fusion(f32[1536,1536]{0,1:T(8,128)S(1)} %convolution_multiply_fusion, f32[1536,1536]{1,0:T(8,128)} %bitcast.21, f32[1536]{0:T(1024)S(1)} %get-tuple-element.6), kind=kOutput, calls=%fused_computation.3 | convolution fusion | flops 21757427712 | bytes 37754880 | tf_op jit(solution)/shard_map/dot_general | solution.py:20
  120.6 0.0 copy-done
  120.6 238.8 %panel_reduce.1 = (f32[192,3072]{1,0:T(8,128)}, f32[2,192,1536]{2,1,0:T(8,128)}) custom-call(bf16[1536,1536]{1,0:T(8,128)(2,1)} %get-tuple-element.9.refs_0_, bf16[1536,1536]{1,0:T(8,128)(2,1)} %get-tuple-element.8.refs_1_, f32[1536,3072]{1,0:T(8,128)} %refs_2_.1), custom_call_target="tpu_custom_call" | custom-call | tf_op jit(solution)/shard_map/panel_reduce/pallas_call | solution.py:311
  359.5 0.0 copy-done.6
  359.5 2.2 bitcast_select_fusion
  361.7 0.0 copy-start.2
  361.7 8.8 %fusion.34 = f32[384,1536]{1,0:T(8,128)S(1)} fusion(f32[384,1536]{1,0:T(8,128)S(1)} %get-tuple-element.11, f32[1536,1536]{0,1:T(8,128)} %copy-done), kind=kOutput, calls=%fused_computation.61 | convolution fusion | flops 5435817984 | bytes 14155776 | tf_op jit(solution)/shard_map/dot_general | solution.py:20
  370.5 0.0 copy-done.2
  370.5 0.0 copy-start.1
  370.5 6.4 %convolution_subtract_fusion = f32[384,1536]{1,0:T(8,128)S(1)} fusion(f32[384,1536]{1,0:T(8,128)S(1)} %fusion.34, f32[384,1536]{1,0:T(8,128)S(1)} %get-tuple-element.10, f32[1536,1536]{0,1:T(8,128)S(1)} %copy-done.2), kind=kOutput, calls=%fused_computation.9 | convolution fusion | flops 5436407808 | bytes 16515072 | tf_op jit(solution)/shard_map/dot_general | solution.py:20
  377.0 0.7 fusion.32
  377.6 0.0 collective-permute-done
  377.6 0.0 collective-permute-done.1
  377.6 0.0 copy-done.1
  377.6 3.7 convolution_add_fusion
  381.4 2.6 reshape.75
  384.0 1.6 copy.23
  385.6 34.3 %block_reduce.1 = f32[192,384]{1,0:T(8,128)} custom-call(f32[4,2,192,384]{3,2,1,0:T(8,128)} %bitcast.24), custom_call_target="tpu_custom_call" | custom-call | tf_op jit(solution)/shard_map/block_reduce/pallas_call | solution.py:337
  419.9 1.6 collective-permute-start.2
  421.5 0.0 copy-done.5
  421.5 0.0 copy-done.8
  421.5 1.1 negate_select_fusion
  422.6 0.2 constant_dynamic-slice_fusion.1
  422.8 0.1 collective-permute-start.3
  422.9 1.4 collective-permute-done.3
  424.3 3.9 fusion.7.part
  428.2 24.3 %plane_reduce.1 = f32[192,384]{1,0:T(8,128)} custom-call(f32[192,1536]{1,0:T(8,128)} %fusion.7.part), custom_call_target="tpu_custom_call" | custom-call | tf_op jit(solution)/shard_map/plane_reduce/pallas_call | solution.py:386
  452.5 0.0 collective-permute-done.2
  452.5 1.8 fusion.20
  454.3 3.3 copy.25
  (13 shorter events, 0.0 us)
Async XLA Ops:
  2.5 357.0 %copy-start.6 = (pred[384]{0:T(512)(128)(4,1)}, pred[384]{0:T(512)(128)(4,1)S(1)}, u32[]{:S(2)}) copy-start(pred[384]{0:T(512)(128)(4,1)S(1)} %dynamic_slice.35) | copy-start | bytes 1156
  5.1 372.5 %collective-permute-start = (f32[192,192]{1,0:T(8,128)}, f32[192,192]{1,0:T(8,128)}, u32[]{:S(2)}, u32[]{:S(2)}) collective-permute-start(f32[192,192]{1,0:T(8,128)} %get-tuple-element.14), channel_id=1, source_target_pairs={{0,0},{1,1},{2,8},{3,9},{4,16},{5,17},{6,24},{7,25},{8,2},{9,3},{1... | collective-permute-start | bytes 442376 | tf_op jit(solution)/shard_map/ppermute | solution.py:643
  8.1 369.5 %collective-permute-start.1 = (f32[192,192]{1,0:T(8,128)}, f32[192,192]{1,0:T(8,128)}, u32[]{:S(2)}, u32[]{:S(2)}) collective-permute-start(f32[192,192]{1,0:T(8,128)} %get-tuple-element.15), channel_id=1, source_target_pairs={{0,1},{1,0},{2,9},{3,8},{4,17},{5,16},{6,25},{7,24},{8,3},{9,2},{1... | collective-permute-start | bytes 442376 | tf_op jit(solution)/shard_map/ppermute | solution.py:643
  11.2 61.6 %copy-start.9 = (s32[8,24]{1,0:T(8,128)S(1)}, s32[8,24]{1,0:T(8,128)}, u32[]{:S(2)}) copy-start(s32[8,24]{1,0:T(8,128)} %param.13) | copy-start | bytes 2308
  88.7 31.9 %copy-start = (f32[1536,1536]{0,1:T(8,128)}, f32[1536,1536]{0,1:T(8,128)S(1)}, u32[]{:S(2)}) copy-start(f32[1536,1536]{0,1:T(8,128)S(1)} %convolution_multiply_fusion) | copy-start | bytes 28311556
  361.7 8.8 %copy-start.2 = (f32[1536,1536]{0,1:T(8,128)S(1)}, f32[1536,1536]{0,1:T(8,128)}, u32[]{:S(2)}) copy-start(f32[1536,1536]{0,1:T(8,128)} %get-tuple-element.20) | copy-start | bytes 28311556
  370.5 7.1 %copy-start.1 = (f32[192,1536]{1,0:T(8,128)S(1)}, f32[192,1536]{1,0:T(8,128)}, u32[]{:S(2)}) copy-start(f32[192,1536]{1,0:T(8,128)} %and_select_fusion) | copy-start | bytes 3538948
  385.6 36.0 %copy-start.5 = (s32[384]{0:T(512)S(1)}, s32[384]{0:T(512)}, u32[]{:S(2)}) copy-start(s32[384]{0:T(512)} %get-tuple-element.17) | copy-start | bytes 4612
  385.6 36.0 %copy-start.8 = (s32[192]{0:T(256)S(1)}, s32[192]{0:T(256)}, u32[]{:S(2)}) copy-start(s32[192]{0:T(256)} %get-tuple-element.18) | copy-start | bytes 2308
  419.9 32.6 %collective-permute-start.2 = (f32[192,384]{1,0:T(8,128)}, f32[192,384]{1,0:T(8,128)S(1)}, u32[]{:S(2)}, u32[]{:S(2)}) collective-permute-start(f32[192,384]{1,0:T(8,128)} %block_reduce.1), channel_id=1, source_target_pairs={{0,0},{1,1},{2,8},{3,9},{4,16},{5,17},{6,24},{7,25},{8,2},{9,3},{1... | collective-permute-start | bytes 884744 | tf_op jit(solution)/shard_map/ppermute | solution.py:643
  422.8 1.5 collective-permute-start.3
  424.3 28.2 %copy-start.3 = (f32[192,384]{1,0:T(8,128)S(1)}, f32[192,384]{1,0:T(8,128)}, u32[]{:S(2)}) copy-start(f32[192,384]{1,0:T(8,128)} %param.10) | copy-start | bytes 884740
  424.3 28.2 %copy-start.4 = (s32[384]{0:T(512)S(1)}, s32[384]{0:T(512)}, u32[]{:S(2)}) copy-start(s32[384]{0:T(512)} %get-tuple-element.16) | copy-start | bytes 4612
  424.3 28.2 %copy-start.7 = (pred[384]{0:T(512)(128)(4,1)S(1)}, pred[384]{0:T(512)(128)(4,1)}, u32[]{:S(2)}) copy-start(pred[384]{0:T(512)(128)(4,1)} %copy-done.6) | copy-start | bytes 1156

commit v2 on v1

--- a/solution.py
+++ b/solution.py
@@ -45,8 +45,10 @@
 
 def line_kernel(chunks, chips, width, deal, *refs):
     if deal:
-        high, low, known, panel, dealt, own, pair, below, above, sems, *refs = refs
-        deal_send, deal_recv, fetched, known_high, known_low, sent, fetch = refs
+        high, low, known, sep, lead, start, upper, panel, product, *refs = refs
+        own, pair, below, above, sems, *refs = refs
+        deal_send, deal_recv, fetched, known_high, known_low, sent, fetch, *refs = refs
+        dealt, factors, total, factor_sems, total_sem = refs
     else:
         part, panel, own, pair, below, above, sems = refs
     load, pair_send, pair_recv, up_send, up_recv, down_send, down_recv, store = (
@@ -125,7 +127,7 @@
         return (chip == row) & (j // half == core)
 
     def deal_spot(j):
-        return dealt.at[core, :, span(j % half)]
+        return dealt.at[core, j % half]
 
     def deal_copy(j):
         return remote(
@@ -133,8 +135,19 @@
             (chip, 2 * row + j // half),
         )
 
-    def keep_copy(j):
-        return pltpu.make_async_copy(own.at[j, chip], deal_spot(j), deal_recv.at[core, j % half])
+    def factor_copies(a):
+        slot = a % 2
+        at = pl.ds(pl.multiple_of(a * width, width), width)
+        return [
+            pltpu.make_async_copy(
+                source.at[at, :], factors.at[slot, pl.ds(i * width, width)], factor_sems.at[slot, i]
+            )
+            for i, source in enumerate((sep, lead))
+        ]
+
+    def halves(x):
+        rounded = x.astype(jnp.bfloat16)
+        return rounded, (x - rounded.astype(jnp.float32)).astype(jnp.bfloat16)
 
     def begin(j, carry):
         load_copy(j).start()
@@ -143,6 +156,11 @@
 
     if deal:
         fetch_copy(0).start()
+        for copy in factor_copies(0):
+            copy.start()
+        total_copy = pltpu.make_async_copy(start, total, total_sem.at[0])
+        total_copy.start()
+        total_copy.wait()
     else:
         lax.fori_loop(0, chunks, begin, 0)
 
@@ -187,6 +205,39 @@
 
         lax.fori_loop(0, chips, unit, 0)
 
+    def accumulate(a):
+        for i, copy in enumerate(factor_copies(a)):
+            copy.wait()
+
+        @pl.when(a + 1 < half)
+        def _():
+            for copy in factor_copies(a + 1):
+                copy.start()
+
+        for side in range(2):
+
+            @pl.when(jnp.logical_not((chip == row) & (core == side)))
+            def _():
+                remote(
+                    own.at[0, 0], dealt.at[side, a], deal_send.at[0], deal_recv.at[side, a],
+                    (row, other),
+                ).wait_recv()
+
+        moved = jnp.concatenate([dealt[0, a], dealt[1, a]], axis=0)
+        raised = moved * upper[...]
+        moved_high, moved_low = halves(jnp.concatenate([moved - raised, -raised], axis=1))
+
+        def column(n, carry):
+            at = pl.ds(pl.multiple_of(n * 2 * width, 2 * width), 2 * width)
+            factor_high, factor_low = halves(factors[a % 2, :, at])
+            term = jnp.dot(moved_high, factor_low, preferred_element_type=jnp.float32)
+            term += jnp.dot(moved_low, factor_high, preferred_element_type=jnp.float32)
+            term += jnp.dot(moved_high, factor_high, preferred_element_type=jnp.float32)
+            total[:, at] += term
+            return carry
+
+        lax.fori_loop(0, total.shape[1] // (2 * width), column, 0)
+
     def tick(t, carry):
         if deal:
 
@@ -246,15 +297,22 @@
 
                 @pl.when(kept(ready))
                 def _():
-                    keep_copy(ready).start()
+                    dealt[core, ready % half] = own[ready, chip]
 
                 @pl.when(jnp.logical_not(kept(ready)))
                 def _():
                     deal_copy(ready).start()
 
+        if deal:
+            arrival = sum_at - jnp.maximum(row, last - row) - 2 - core * half
+
+            @pl.when((arrival >= 0) & (arrival < half))
+            def _():
+                accumulate(arrival)
+
         return carry
 
-    lax.fori_loop(0, chunks + last + lag, tick, 0)
+    lax.fori_loop(0, chunks + last + 2 * lag, tick, 0)
 
     def finish(j, carry):
         @pl.when(j >= (chunks - 4 if deal else 0))
@@ -281,16 +339,13 @@
 
     lax.fori_loop(0, chunks, finish, 0)
     if deal:
-
-        def landed(i, carry):
-            spot = dealt.at[i // half, :, span(i % half)]
-            pltpu.make_async_copy(own.at[0, 0], spot, deal_recv.at[i // half, i % half]).wait()
-            return carry
-
-        lax.fori_loop(0, 2 * half, landed, 0)
+        total_copy = pltpu.make_async_copy(total, product, total_sem.at[0])
+        total_copy.start()
+        total_copy.wait()
 
 
 ANYWHERE = pl.BlockSpec(memory_space=pl.ANY)
+IN_VMEM = pl.BlockSpec(memory_space=pltpu.VMEM)
 
 
 def line_params(number):
@@ -304,17 +359,18 @@
     return [block] * 4 + [pltpu.SemaphoreType.DMA((8, chunks))]
 
 
-def panel_reduce(high, low, known, chips, depth):
+def panel_reduce(high, low, known, sep, lead, start, upper, chips):
     inner, wide = known.shape
+    depth = start.shape[0] // 2
     width = 128
     chunks = wide // width
     return pl.pallas_call(
         functools.partial(line_kernel, chunks, chips, width, True),
         out_shape=[
             jax.ShapeDtypeStruct((depth, wide), jnp.float32),
-            jax.ShapeDtypeStruct((2, depth, wide // 2), jnp.float32),
+            jax.ShapeDtypeStruct(start.shape, jnp.float32),
         ],
-        in_specs=[pl.BlockSpec(memory_space=pltpu.VMEM)] * 2 + [ANYWHERE],
+        in_specs=[IN_VMEM] * 2 + [ANYWHERE] * 4 + [IN_VMEM],
         out_specs=[ANYWHERE] * 2,
         scratch_shapes=line_scratch(chunks, chips, depth, width)
         + [
@@ -325,10 +381,15 @@
             pltpu.VMEM((inner, 2 * width), jnp.bfloat16),
             pltpu.VMEM((4, chips, depth, width), jnp.float32),
             pltpu.SemaphoreType.DMA((2,)),
+            pltpu.VMEM((2, chunks // 2, depth, width), jnp.float32),
+            pltpu.VMEM((2, 2 * width, start.shape[1]), jnp.float32),
+            pltpu.VMEM(start.shape, jnp.float32),
+            pltpu.SemaphoreType.DMA((2, 2)),
+            pltpu.SemaphoreType.DMA((1,)),
         ],
         compiler_params=line_params(1),
         name="panel_reduce",
-    )(high, low, known)
+    )(high, low, known, sep, lead, start, jnp.broadcast_to(upper[:, None], (2 * depth, width)))
 
 
 def block_reduce(part):
@@ -405,7 +466,7 @@
     core = col % 2
     other = col + 1 - 2 * core
     last = chips - 1
-    piece = held.shape[2]
+    piece = held.shape[2] // 2
     along_x, along_y, across = row + 1 - 2 * (row % 2), (row + 2) % 4, 3 - row
 
     barrier = pltpu.get_barrier_semaphore()
@@ -428,40 +489,40 @@
     met = 3 + (chip > 0).astype(jnp.int32) + (chip < last).astype(jnp.int32)
     pl.semaphore_wait(barrier, met)
 
-    def remote(ref, send, recv, spot, device):
+    def remote(at, quarter, side, send, recv, device):
+        ref = held.at[2 * at + core, quarter, pl.ds(side * piece, piece)]
+        spot = 2 * at + side
         return pltpu.make_async_remote_copy(
             src_ref=ref, dst_ref=ref, send_sem=sems.at[send, spot], recv_sem=sems.at[recv, spot],
             device_id=device, device_id_type=MESH,
         )
 
-    def item(at, quarter):
-        return held.at[2 * at + core, quarter]
-
-    def up(at):
-        return remote(item(at, row), 0, 2, at, (row, col + 2))
-
-    def down(at):
-        return remote(item(at, row), 1, 2, at, (row, col - 2))
-
-    def sideways_x(at):
-        return remote(item(at, row), 3, 4, at, (along_x, col))
-
-    def sideways_y(at):
-        return remote(item(at, row), 5, 6, at, (along_y, col))
+    def up(at, side):
+        return remote(at, row, side, 0, 2, (row, col + 2))
+
+    def down(at, side):
+        return remote(at, row, side, 1, 2, (row, col - 2))
+
+    def sideways_x(at, side):
+        return remote(at, row, side, 3, 4, (along_x, col))
+
+    def sideways_y(at, side):
+        return remote(at, row, side, 5, 6, (along_y, col))
 
     def onward_x(at):
-        return remote(item(at, along_y).at[pl.ds(0, piece // 2)], 7, 8, at, (along_x, col))
+        return remote(at, along_y, 0, 7, 8, (along_x, col))
 
     def onward_y(at):
-        return remote(
-            item(at, along_x).at[pl.ds(piece // 2, piece // 2)], 9, 10, at, (along_y, col)
+        return remote(at, along_x, 1, 7, 8, (along_y, col))
+
+    def hand(at, quarter, side):
+        return remote(at, quarter, side, 9 + quarter, 13 + quarter, (row, other))
+
+    def hand_own():
+        return pltpu.make_async_remote_copy(
+            src_ref=held.at[col], dst_ref=held.at[col], send_sem=sems.at[17, 0],
+            recv_sem=sems.at[18, 0], device_id=(row, other), device_id_type=MESH,
         )
-
-    def hand(at, quarter):
-        return remote(item(at, quarter), 11 + quarter, 15 + quarter, at, (row, other))
-
-    def hand_own():
-        return remote(held.at[col], 19, 20, 0, (row, other))
 
     def keep(c):
         return pltpu.make_async_copy(held.at[c], out.at[c], stores.at[c])
@@ -477,57 +538,59 @@
             def _():
                 visit(chip + distance, False)
 
-    load = pltpu.make_async_copy(mine, held.at[col], sems.at[21, 0])
+    load = pltpu.make_async_copy(mine, held.at[col], sems.at[19, 0])
     load.start()
     load.wait()
 
-    @pl.when(chip < last)
-    def _():
-        up(chip).start()
-
-    @pl.when(chip > 0)
-    def _():
-        down(chip).start()
-
+    def send_line(at, side, rising):
+        if rising:
+
+            @pl.when(chip < last)
+            def _():
+                up(at, side).start()
+
+        else:
+
+            @pl.when(chip > 0)
+            def _():
+                down(at, side).start()
+
+    for side in range(2):
+        send_line(chip, side, True)
+        send_line(chip, side, False)
     hand_own().start()
     keep(col).start()
 
     def from_line(at, rising):
-        if rising:
-            up(at).wait_recv()
-
-            @pl.when(chip < last)
-            def _():
-                up(at).start()
-
-        else:
-            down(at).wait_recv()
-
-            @pl.when(chip > 0)
-            def _():
-                down(at).start()
-
-        sideways_x(at).start()
-        sideways_y(at).start()
-        hand(at, row).start()
+        for side in range(2):
+            up(at, side).wait_recv()
+            send_line(at, side, rising)
+            sideways_x(at, side).start()
+            sideways_y(at, side).start()
+            hand(at, row, side).start()
 
     def from_sides(at, rising):
-        sideways_x(at).wait_recv()
-        onward_y(at).start()
-        hand(at, along_x).start()
-        sideways_y(at).wait_recv()
-        onward_x(at).start()
-        hand(at, along_y).start()
+        for side in range(2):
+            sideways_x(at, side).wait_recv()
+            if side == 1:
+                onward_y(at).start()
+            sideways_y(at, side).wait_recv()
+            if side == 0:
+                onward_x(at).start()
+            hand(at, along_x, side).start()
+            hand(at, along_y, side).start()
 
     def from_across(at, rising):
         onward_x(at).wait_recv()
+        hand(at, across, 0).start()
         onward_y(at).wait_recv()
-        hand(at, across).start()
+        hand(at, across, 1).start()
         keep(2 * at + core).start()
 
     def from_other(at, rising):
         for quarter in range(4):
-            hand(at, quarter).wait_recv()
+            for side in range(2):
+                hand(at, quarter, side).wait_recv()
         keep(2 * at + 1 - core).start()
 
     both_ways(from_line)
@@ -537,34 +600,33 @@
     keep(other).start()
     both_ways(from_other)
 
+    def drain_line(at, side, rising):
+        if rising:
+
+            @pl.when(chip < last)
+            def _():
+                up(at, side).wait_send()
+
+        else:
+
+            @pl.when(chip > 0)
+            def _():
+                down(at, side).wait_send()
+
     def drain(at, rising):
-        if rising:
-
-            @pl.when(chip < last)
-            def _():
-                up(at).wait_send()
-
-        else:
-
-            @pl.when(chip > 0)
-            def _():
-                down(at).wait_send()
-
-        for copy in (sideways_x, sideways_y, onward_x, onward_y):
-            copy(at).wait_send()
-        for quarter in range(4):
-            hand(at, quarter).wait_send()
+        for side in range(2):
+            drain_line(at, side, rising)
+            sideways_x(at, side).wait_send()
+            sideways_y(at, side).wait_send()
+            for quarter in range(4):
+                hand(at, quarter, side).wait_send()
+        onward_x(at).wait_send()
+        onward_y(at).wait_send()
 
     both_ways(drain)
-
-    @pl.when(chip < last)
-    def _():
-        up(chip).wait_send()
-
-    @pl.when(chip > 0)
-    def _():
-        down(chip).wait_send()
-
+    for side in range(2):
+        drain_line(chip, side, True)
+        drain_line(chip, side, False)
     hand_own().wait_send()
     for c in range(2 * chips):
         keep(c).wait()
@@ -583,13 +645,91 @@
         out_specs=ANYWHERE,
         scratch_shapes=[
             pltpu.VMEM(shape, jnp.float32),
-            pltpu.SemaphoreType.DMA((22, cols // 2)),
+            pltpu.SemaphoreType.DMA((20, cols)),
             pltpu.SemaphoreType.DMA((cols,)),
         ],
         compiler_params=line_params(4),
         name="gather_rows",
     )(mine.reshape(4, piece, wide))
     return out.reshape(cols * depth, wide)
+
+
+def lead_kernel(tile, flags, factor, listed, upper, coupling, high, low, lead, sep, *scratch):
+    upper_high, upper_low, total = scratch
+    wide = factor.shape[1]
+    block = factor.shape[0] // listed.shape[1]
+
+    for i in range(listed.shape[1]):
+        at = pl.ds(i * block, block)
+        sep[at, :] = factor[at, :] * listed[0, i : i + 1, :]
+
+    def split(x):
+        rounded = x.astype(jnp.bfloat16)
+        return rounded, (x - rounded.astype(jnp.float32)).astype(jnp.bfloat16)
+
+    def prepare(k, carry):
+        at = pl.ds(pl.multiple_of(k * tile, tile), tile)
+        upper_high[:, at], upper_low[:, at] = split(sep[:, at] * upper[:, at])
+        return carry
+
+    lax.fori_loop(0, wide // tile, prepare, 0)
+
+    def column(m, carry):
+        at = pl.ds(pl.multiple_of(m * tile, tile), tile)
+        total[...] = -sep[:, at]
+
+        def inner(k, carry):
+            @pl.when(flags[k, m] != 0)
+            def _():
+                along = pl.ds(pl.multiple_of(k * tile, tile), tile)
+                pair_high, pair_low = split(coupling[along, at])
+
+                def times(left, right):
+                    return jnp.dot(left[:, along], right, preferred_element_type=jnp.float32)
+
+                term = times(upper_high, pair_low) + times(upper_low, pair_high)
+                total[...] += term + times(upper_high, pair_high)
+
+            return carry
+
+        lax.fori_loop(0, wide // tile, inner, 0)
+        lead[:, at] = total[...]
+        high[at, :], low[at, :] = split(total[...].T)
+        return carry
+
+    lax.fori_loop(0, wide // tile, column, 0)
+
+
+def lead_factors(factor, listed, upper, coupling, flags):
+    tall, wide = factor.shape
+    block = tall // listed.shape[0]
+    step = 2 * block
+    tile = wide // flags.shape[0]
+    turned = pl.BlockSpec((wide, step), lambda i, f: (0, i))
+    straight = pl.BlockSpec((step, wide), lambda i, f: (i, 0))
+    return pl.pallas_call(
+        functools.partial(lead_kernel, tile),
+        out_shape=[jax.ShapeDtypeStruct((wide, tall), jnp.bfloat16)] * 2
+        + [jax.ShapeDtypeStruct((tall, wide), jnp.float32)] * 2,
+        grid_spec=pltpu.PrefetchScalarGridSpec(
+            num_scalar_prefetch=1,
+            grid=(tall // step,),
+            in_specs=[
+                straight,
+                pl.BlockSpec((1, 2, wide), lambda i, f: (i, 0, 0)),
+                pl.BlockSpec((1, wide), lambda i, f: (0, 0)),
+                pl.BlockSpec((wide, wide), lambda i, f: (0, 0), pipeline_mode=pl.Buffered(1)),
+            ],
+            out_specs=[turned, turned, straight, straight],
+            scratch_shapes=[
+                pltpu.VMEM((step, wide), jnp.bfloat16),
+                pltpu.VMEM((step, wide), jnp.bfloat16),
+                pltpu.VMEM((step, tile), jnp.float32),
+            ],
+        ),
+        compiler_params=pltpu.CompilerParams(vmem_limit_bytes=62 << 20),
+        name="lead_factors",
+    )(flags, factor, listed.reshape(-1, 2, wide), upper[None, :], coupling)
 
 
 def shards(known_inverse, factor_sep, factor_pair, pivot_inverse, widths, parent_of, ancestors):
@@ -612,11 +752,8 @@
     def cols_of(x, index, size):
         return lax.dynamic_slice_in_dim(x, index * size, size, 1)
 
-    sep_index = col_index * sep_local + jnp.arange(sep_local, dtype=jnp.int32)
-    block_onehot = (
-        (sep_index // (NS // NBLK))[:, None] == jnp.arange(NBLK, dtype=jnp.int32)[None, :]
-    ).astype(jnp.float32)
-    sep_factor = factor_sep * plain_dot(block_onehot, column_blocks.T)
+    blocks = sep_local // (NS // NBLK)
+    listed = lax.dynamic_slice_in_dim(column_blocks, col_index * blocks, blocks, 1).T
     upper_cols = column_upper.astype(jnp.float32)
     owner_rows = rows_of(column_owner, col_index, pair_local)
     owner_wide = rows_of(column_owner, row_index, wide_local)
@@ -654,18 +791,24 @@
     )
     pivot_coupled = plain_dot(pivot_tile, coupling)
 
-    lead = plain_dot(sep_factor * upper_cols[None, :], coupling_all) - sep_factor
-    turned = lead.T
-    high = lax.reduce_precision(turned, 8, 7)
-    low = (turned - high).astype(jnp.bfloat16)
-    panel, dealt = panel_reduce(
-        high.astype(jnp.bfloat16), low, known_inverse, chips, pair_local
-    )
-    moved = dealt.reshape(wide_local, sep_local)
-
-    moved_upper = jnp.where(upper_wide[:, None], moved, 0.0)
-    moved_lower = jnp.where(upper_wide[:, None], 0.0, moved)
-    product = plain_dot(moved_lower, sep_factor) - plain_dot(moved_upper, lead) + pivot_coupled
+    nodes = jnp.arange(NSUP, dtype=jnp.int32)
+    tiles = WTOT // 256
+    holds = jnp.any(column_owner.reshape(tiles, 256, 1) == nodes, axis=1)
+    wants = jnp.any(column_parent.reshape(tiles, 256, 1) == nodes, axis=1)
+    flags = jnp.any(holds[:, None, :] & wants[None, :, :], axis=2).astype(jnp.int32)
+    high, low, lead, sep_factor = lead_factors(
+        factor_sep, listed, upper_cols, coupling_all, flags
+    )
+    panel, product = panel_reduce(
+        high,
+        low,
+        known_inverse,
+        sep_factor,
+        lead,
+        pivot_coupled,
+        upper_wide.astype(jnp.float32),
+        chips,
+    )
     product = product.reshape(2, pair_local, chips, wide_local).transpose(2, 0, 1, 3)
     tile = block_reduce(product)
 

time: 458 us -> 422 us (0.921)
  matrix products: 60.9 us -> 6.66 us
  Pallas kernels: 359 us -> 394 us
  local copies, waits for them, and re-layouts: 19.7 us -> 10.2 us
    dot_general x6 -> x2, matrix products: 57 us -> 2.76 us  [plain_dot(): jnp.dot(left, right, precision=exact_mode, preferred_element_type=jnp.flo...]
    pallas_call x0 -> x1, Pallas kernels: none -> 32.1 us  [lead_factors(): pl.pallas_call(functools.partial(lead_kernel, tile), out_shape=[jax.Shape...]
    unnamed x22 -> x7, local copies, waits for them, and re-layouts: 12.9 us -> 3.31 us
  transfers between devices with their start and end apart: 4 -> 4, of which waited for: 1 -> 1; matrix products, arithmetic and copies ran while one was open for 16% -> 2% of each run, Pallas kernels for 71% -> 27%
where the time goes in v2:
time: 422 us; the launch traced here: 425 us
  Pallas kernels  394 us (93%)
  local copies, waits for them, and re-layouts  10.2 us (2%)
  other arithmetic  8.92 us (2%)
  matrix products  6.66 us (2%)
    pallas_call x1, Pallas kernels, panel_reduce(): pl.pallas_call(functools.partial(line_kernel, chunks, chips, width, True)...  241 us
    pallas_call x1, Pallas kernels, gather_rows(): pl.pallas_call(functools.partial(gather_kernel, cols // 2), out_shape=jax...  59.7 us
    pallas_call x1, Pallas kernels, block_reduce(): pl.pallas_call(functools.partial(line_kernel, chunks, chips, wide // chun...  37.7 us
    pallas_call x1, Pallas kernels, lead_factors(): pl.pallas_call(functools.partial(lead_kernel, tile), out_shape=[jax.Shape...  32.1 us
    pallas_call x1, Pallas kernels, plane_reduce(): pl.pallas_call(functools.partial(plane_kernel, rows), out_shape=jax.Shape...  23.5 us
  transfers between devices with their start and end apart: 4, of which 1 were waited for; matrix products, arithmetic and copies ran while one was open for 2% of the time, Pallas kernels for 27%

profile of v2, /device:TPU:0, one launch (start us, length us, event | category | flops | bytes accessed | tf_op | source)
XLA Modules:
  0.0 424.8 jit_solution(17233467565388147631)
XLA Ops:
  0.6 0.0 copy-start.1
  0.7 0.9 reduce-window.8
  1.6 0.1 convert_reduce_fusion
  1.7 0.1 dynamic_slice.38
  1.8 0.7 select_reduce_fusion
  2.5 0.1 fusion.25
  2.6 0.1 fusion.28
  2.7 1.1 fusion.14
  3.8 0.2 constant_dynamic-slice_fusion.3
  4.0 0.7 collective-permute-start
  4.7 0.6 collective-permute-start.1
  5.2 0.8 fusion.17
  6.0 0.3 fusion.18
  6.3 0.3 fusion.19
  6.6 0.0 copy-done.1
  6.6 1.3 and_select_fusion
  7.9 0.2 and_reduce_fusion
  8.1 0.6 reshape.80.upper
  8.7 0.6 convert_element_type.25.flags
  9.3 0.7 reshape.76.listed
  9.9 59.7 %gather_rows.1 = f32[8,4,48,1536]{3,2,1,0:T(8,128)} custom-call(f32[4,48,1536]{2,1,0:T(8,128)} %bitcast.13), custom_call_target="tpu_custom_call" | custom-call | tf_op jit(solution)/shard_map/gather_rows/pallas_call | solution.py:641
  69.6 0.0 copy-start
  69.6 32.1 %lead_factors.1 = (bf16[1536,1536]{1,0:T(8,128)(2,1)}, bf16[1536,1536]{1,0:T(8,128)(2,1)}, f32[1536,1536]{1,0:T(8,128)}, f32[1536,1536]{1,0:T(8,128)}) custom-call(s32[6,6]{1,0:T(8,128)} %convert_element_type.25.flags, f32[1536,1536]{1,0:T(8,128)} %factor.1, f32[4,2,1536]{2,1,0:T(2,128)} %reshape.76.listed, f32[1,1536]{1,0:T(1,128)} %reshape.80.upper, ...), custom_call_target="tpu_custom_call" | custom-call | tf_op jit(solution)/shard_map/lead_factors/pallas_call | solution.py:710
  101.7 0.1 fusion.27
  101.8 0.0 collective-permute-done
  101.8 0.0 collective-permute-done.1
  101.8 0.0 copy-done
  101.8 2.5 fusion.2.refs_5_
  104.3 0.8 broadcast_in_dim.33.refs_6_
  105.1 240.9 %panel_reduce.1 = (f32[192,3072]{1,0:T(8,128)}, f32[384,1536]{1,0:T(8,128)}) custom-call(bf16[1536,1536]{1,0:T(8,128)(2,1)} %get-tuple-element.8.refs_0_, bf16[1536,1536]{1,0:T(8,128)(2,1)} %get-tuple-element.9.refs_1_, f32[1536,3072]{1,0:T(8,128)} %refs_2_.1, f32[1536,1536]{1,0:T(8,128)} %get-tuple-element.10.refs_3_, ...), custom_call_target="tpu_custom_call" | custom-call | tf_op jit(solution)/shard_map/panel_reduce/pallas_call | solution.py:367
  346.0 2.6 reshape.79
  348.6 1.6 copy.12
  350.2 37.7 %block_reduce.1 = f32[192,384]{1,0:T(8,128)} custom-call(f32[4,2,192,384]{3,2,1,0:T(8,128)} %bitcast.14), custom_call_target="tpu_custom_call" | custom-call | tf_op jit(solution)/shard_map/block_reduce/pallas_call | solution.py:398
  387.9 1.6 collective-permute-start.2
  389.5 1.1 negate_select_fusion
  390.6 0.2 constant_dynamic-slice_fusion.1
  390.8 0.1 collective-permute-start.3
  390.8 1.4 collective-permute-done.3
  392.3 0.0 copy-start.2
  392.3 3.9 fusion.part
  396.2 23.5 %plane_reduce.1 = f32[192,384]{1,0:T(8,128)} custom-call(f32[192,1536]{1,0:T(8,128)} %fusion.part), custom_call_target="tpu_custom_call" | custom-call | tf_op jit(solution)/shard_map/plane_reduce/pallas_call | solution.py:447
  419.6 0.0 collective-permute-done.2
  419.7 0.0 copy-done.2
  419.7 1.8 fusion.13
  421.5 3.3 copy.14
  (5 shorter events, 0.0 us)
Async XLA Ops:
  0.6 6.0 %copy-start.1 = (f32[192,1536]{1,0:T(8,128)S(1)}, f32[192,1536]{1,0:T(8,128)}, u32[]{:S(2)}) copy-start(f32[192,1536]{1,0:T(8,128)} %param.9) | copy-start | bytes 3538948
  4.0 97.8 %collective-permute-start = (f32[192,192]{1,0:T(8,128)S(1)}, f32[192,192]{1,0:T(8,128)S(1)}, u32[]{:S(2)}, u32[]{:S(2)}) collective-permute-start(f32[192,192]{1,0:T(8,128)S(1)} %get-tuple-element.20), channel_id=1, source_target_pairs={{0,0},{1,1},{2,8},{3,9},{4,16},{5,17},{6,24},{7,25},{8,2},{9,3},{1... | collective-permute-start | bytes 442376 | tf_op jit(solution)/shard_map/ppermute | solution.py:780
  4.7 97.1 %collective-permute-start.1 = (f32[192,192]{1,0:T(8,128)S(1)}, f32[192,192]{1,0:T(8,128)S(1)}, u32[]{:S(2)}, u32[]{:S(2)}) collective-permute-start(f32[192,192]{1,0:T(8,128)S(1)} %get-tuple-element.21), channel_id=1, source_target_pairs={{0,1},{1,0},{2,9},{3,8},{4,17},{5,16},{6,25},{7,24},{8,3},{9,2},{1... | collective-permute-start | bytes 442376 | tf_op jit(solution)/shard_map/ppermute | solution.py:780
  69.6 32.2 %copy-start = (f32[192,1536]{1,0:T(8,128)S(1)}, f32[192,1536]{1,0:T(8,128)}, u32[]{:S(2)}) copy-start(f32[192,1536]{1,0:T(8,128)} %and_select_fusion) | copy-start | bytes 3538948
  387.9 31.8 %collective-permute-start.2 = (f32[192,384]{1,0:T(8,128)}, f32[192,384]{1,0:T(8,128)S(1)}, u32[]{:S(2)}, u32[]{:S(2)}) collective-permute-start(f32[192,384]{1,0:T(8,128)} %block_reduce.1), channel_id=1, source_target_pairs={{0,0},{1,1},{2,8},{3,9},{4,16},{5,17},{6,24},{7,25},{8,2},{9,3},{1... | collective-permute-start | bytes 884744 | tf_op jit(solution)/shard_map/ppermute | solution.py:780
  390.8 1.5 collective-permute-start.3
  392.3 27.4 %copy-start.2 = (f32[192,384]{1,0:T(8,128)S(1)}, f32[192,384]{1,0:T(8,128)}, u32[]{:S(2)}) copy-start(f32[192,384]{1,0:T(8,128)} %param.10) | copy-start | bytes 884740

commit v3 on v2

--- a/solution.py
+++ b/solution.py
@@ -31,7 +31,8 @@
 
 def supernode_tables(widths, parent_of, ancestors):
     position = jnp.arange(WTOT, dtype=jnp.int32)
-    width_ends = jnp.cumsum(widths)
+    earlier = jnp.arange(NSUP)[None, :] <= jnp.arange(NSUP)[:, None]
+    width_ends = jnp.sum(jnp.where(earlier, widths[None, :], 0), axis=1)
     column_owner = jnp.sum((width_ends[None, :] <= position[:, None]).astype(jnp.int32), axis=1)
     owner_onehot = column_owner[:, None] == jnp.arange(NSUP, dtype=jnp.int32)[None, :]
     listed = jnp.any(
@@ -50,7 +51,8 @@
         deal_send, deal_recv, fetched, known_high, known_low, sent, fetch, *refs = refs
         dealt, factors, total, factor_sems, total_sem = refs
     else:
-        part, panel, own, pair, below, above, sems = refs
+        part, panel, own, pair, below, above, sems, unit_sems = refs
+        flat = len(part.shape) == 3
     load, pair_send, pair_recv, up_send, up_recv, down_send, down_recv, store = (
         sems.at[i] for i in range(8)
     )
@@ -88,15 +90,24 @@
             greet((chip, 2 * row + 1))
 
         met = met + 2 * (chip != row).astype(jnp.int32)
-    pl.semaphore_wait(barrier, met)
-
     def span(j):
         if chunks == 1:
             return pl.ds(0, width)
         return pl.ds(pl.multiple_of(j * width, width), width)
 
-    def load_copy(j):
-        return pltpu.make_async_copy(part.at[:, core, :, span(j)], own.at[j], load.at[j])
+    def unit_span(j, d):
+        at = d * panel.shape[1] + j * width
+        return pl.ds(pl.multiple_of(at, width), width)
+
+    def load_copies(j):
+        if flat:
+            return [
+                pltpu.make_async_copy(
+                    part.at[core, :, unit_span(j, d)], own.at[j, d], unit_sems.at[0, j, d]
+                )
+                for d in range(chips)
+            ]
+        return [pltpu.make_async_copy(part.at[:, core, :, span(j)], own.at[j], load.at[j])]
 
     def remote(src, dst, send, recv, device):
         return pltpu.make_async_remote_copy(
@@ -104,9 +115,17 @@
             device_id=device, device_id_type=MESH,
         )
 
-    def pair_copy(j):
+    def pair_copies(j):
+        if not deal and flat:
+            return [
+                remote(
+                    part.at[1 - core, :, unit_span(j, d)], pair.at[j, d],
+                    unit_sems.at[1, j, d], unit_sems.at[2, j, d], (row, other),
+                )
+                for d in range(chips)
+            ]
         source = sent.at[j % 4] if deal else part.at[:, 1 - core, :, span(j)]
-        return remote(source, pair.at[j], pair_send.at[j], pair_recv.at[j], (row, other))
+        return [remote(source, pair.at[j], pair_send.at[j], pair_recv.at[j], (row, other))]
 
     def fetch_copy(g):
         columns = pl.ds(pl.multiple_of(2 * g * width, 2 * width), 2 * width)
@@ -149,20 +168,21 @@
         rounded = x.astype(jnp.bfloat16)
         return rounded, (x - rounded.astype(jnp.float32)).astype(jnp.bfloat16)
 
-    def begin(j, carry):
-        load_copy(j).start()
-        pair_copy(j).start()
-        return carry
-
     if deal:
         fetch_copy(0).start()
         for copy in factor_copies(0):
             copy.start()
         total_copy = pltpu.make_async_copy(start, total, total_sem.at[0])
         total_copy.start()
-        total_copy.wait()
+        pl.semaphore_wait(barrier, met)
     else:
-        lax.fori_loop(0, chunks, begin, 0)
+        for j in range(chunks):
+            for copy in load_copies(j):
+                copy.start()
+        pl.semaphore_wait(barrier, met)
+        for j in range(chunks):
+            for copy in pair_copies(j):
+                copy.start()
 
     def multiply(t):
         g = t // 2
@@ -174,8 +194,8 @@
 
         @pl.when(t >= 4)
         def _():
-            pair_copy(t - 4).wait_send()
-            pair_copy(t - 3).wait_send()
+            for copy in pair_copies(t - 4) + pair_copies(t - 3):
+                copy.wait_send()
 
         def split(i, carry):
             at = pl.ds(pl.multiple_of(i * 2 * width, 2 * width), 2 * width)
@@ -206,6 +226,10 @@
         lax.fori_loop(0, chips, unit, 0)
 
     def accumulate(a):
+        @pl.when(a == 0)
+        def _():
+            total_copy.wait()
+
         for i, copy in enumerate(factor_copies(a)):
             copy.wait()
 
@@ -250,16 +274,18 @@
         @pl.when((sum_at >= 0) & (sum_at < chunks))
         def _():
             if not deal:
-                load_copy(sum_at).wait()
-            pair_copy(sum_at).wait_recv()
+                for copy in load_copies(sum_at):
+                    copy.wait()
+            for copy in pair_copies(sum_at):
+                copy.wait_recv()
             own[sum_at] = own[sum_at] + pair[sum_at]
 
         if deal:
 
             @pl.when((t < chunks) & (t % 2 == 0))
             def _():
-                pair_copy(t).start()
-                pair_copy(t + 1).start()
+                for copy in pair_copies(t) + pair_copies(t + 1):
+                    copy.start()
 
         up = sum_at - chip
         down = sum_at - (last - chip)
@@ -317,7 +343,8 @@
     def finish(j, carry):
         @pl.when(j >= (chunks - 4 if deal else 0))
         def _():
-            pair_copy(j).wait_send()
+            for copy in pair_copies(j):
+                copy.wait_send()
 
         store_copy(j).wait()
         for at in range(chips):
@@ -392,15 +419,23 @@
     )(high, low, known, sep, lead, start, jnp.broadcast_to(upper[:, None], (2 * depth, width)))
 
 
-def block_reduce(part):
-    chips, _, depth, wide = part.shape
-    chunks = wide // 128 if wide % 128 == 0 else 1
+def block_reduce(product, chips):
+    tall, wide = product.shape
+    depth, wide = tall // 2, wide // chips
+    if wide % 128:
+        part = product.reshape(2, depth, chips, wide).transpose(2, 0, 1, 3)
+        width = wide
+    else:
+        part = product.reshape(2, depth, chips * wide)
+        width = 128
+    chunks = wide // width
     return pl.pallas_call(
-        functools.partial(line_kernel, chunks, chips, wide // chunks, False),
+        functools.partial(line_kernel, chunks, chips, width, False),
         out_shape=jax.ShapeDtypeStruct((depth, wide), jnp.float32),
         in_specs=[ANYWHERE],
         out_specs=ANYWHERE,
-        scratch_shapes=line_scratch(chunks, chips, depth, wide // chunks),
+        scratch_shapes=line_scratch(chunks, chips, depth, width)
+        + [pltpu.SemaphoreType.DMA((3, chunks, chips))],
         compiler_params=line_params(2),
         name="block_reduce",
     )(part)
@@ -809,8 +844,7 @@
         upper_wide.astype(jnp.float32),
         chips,
     )
-    product = product.reshape(2, pair_local, chips, wide_local).transpose(2, 0, 1, 3)
-    tile = block_reduce(product)
+    tile = block_reduce(product, chips)
 
     dealt_tile = permute(tile, straight)
     pair_tile = jnp.where(

time: 422 us -> 417 us (0.988)
  no operation moved by 1% of the time
where the time goes in v3:
time: 417 us; the launch traced here: 418 us
  Pallas kernels  391 us (94%)
  other arithmetic  8.86 us (2%)
  matrix products  6.66 us (2%)
  local copies, waits for them, and re-layouts  5.99 us (1%)
    pallas_call x1, Pallas kernels, panel_reduce(): pl.pallas_call(functools.partial(line_kernel, chunks, chips, width, True)...  237 us
    pallas_call x1, Pallas kernels, gather_rows(): pl.pallas_call(functools.partial(gather_kernel, cols // 2), out_shape=jax...  59.7 us
    pallas_call x1, Pallas kernels, block_reduce(): pl.pallas_call(functools.partial(line_kernel, chunks, chips, width, False...  39.9 us
    pallas_call x1, Pallas kernels, lead_factors(): pl.pallas_call(functools.partial(lead_kernel, tile), out_shape=[jax.Shape...  32.1 us
    pallas_call x1, Pallas kernels, plane_reduce(): pl.pallas_call(functools.partial(plane_kernel, rows), out_shape=jax.Shape...  22.1 us
  transfers between devices with their start and end apart: 4, of which 1 were waited for; matrix products, arithmetic and copies ran while one was open for 2% of the time, Pallas kernels for 27%

profile of v3, /device:TPU:0, one launch (start us, length us, event | category | flops | bytes accessed | tf_op | source)
XLA Modules:
  0.0 418.0 jit_solution(1832256337928673485)
XLA Ops:
  0.6 0.0 copy-start.1
  0.7 0.9 select_reduce_fusion.1
  1.5 0.1 convert_reduce_fusion
  1.6 0.1 dynamic_slice.38
  1.7 0.7 select_reduce_fusion
  2.5 0.1 fusion.25
  2.6 0.1 fusion.28
  2.6 1.1 fusion.14
  3.7 0.2 constant_dynamic-slice_fusion.2
  3.9 0.7 collective-permute-start
  4.6 0.6 collective-permute-start.1
  5.2 0.8 fusion.17
  6.0 0.3 fusion.18
  6.2 0.3 fusion.19
  6.5 0.0 copy-done.1
  6.5 1.3 and_select_fusion
  7.8 0.2 and_reduce_fusion
  8.0 0.6 reshape.56.upper
  8.6 0.6 convert_element_type.25.flags
  9.2 0.7 reshape.52.listed
  9.9 59.7 %gather_rows.1 = f32[8,4,48,1536]{3,2,1,0:T(8,128)} custom-call(f32[4,48,1536]{2,1,0:T(8,128)} %bitcast.9), custom_call_target="tpu_custom_call" | custom-call | tf_op jit(solution)/shard_map/gather_rows/pallas_call | solution.py:676
  69.6 0.0 copy-start
  69.6 32.1 %lead_factors.1 = (bf16[1536,1536]{1,0:T(8,128)(2,1)}, bf16[1536,1536]{1,0:T(8,128)(2,1)}, f32[1536,1536]{1,0:T(8,128)}, f32[1536,1536]{1,0:T(8,128)}) custom-call(s32[6,6]{1,0:T(8,128)} %convert_element_type.25.flags, f32[1536,1536]{1,0:T(8,128)} %factor.1, f32[4,2,1536]{2,1,0:T(2,128)} %reshape.52.listed, f32[1,1536]{1,0:T(1,128)} %reshape.56.upper, ...), custom_call_target="tpu_custom_call" | custom-call | tf_op jit(solution)/shard_map/lead_factors/pallas_call | solution.py:745
  101.7 0.1 fusion.27
  101.8 0.0 collective-permute-done
  101.8 0.0 collective-permute-done.1
  101.8 0.0 copy-done
  101.8 2.5 fusion.2.refs_5_
  104.3 0.8 broadcast_in_dim.47.refs_6_
  105.1 237.5 %panel_reduce.1 = (f32[192,3072]{1,0:T(8,128)}, f32[384,1536]{1,0:T(8,128)}) custom-call(bf16[1536,1536]{1,0:T(8,128)(2,1)} %get-tuple-element.8.refs_0_, bf16[1536,1536]{1,0:T(8,128)(2,1)} %get-tuple-element.9.refs_1_, f32[1536,3072]{1,0:T(8,128)} %refs_2_.1, f32[1536,1536]{1,0:T(8,128)} %get-tuple-element.10.refs_3_, ...), custom_call_target="tpu_custom_call" | custom-call | tf_op jit(solution)/shard_map/panel_reduce/pallas_call | solution.py:394
  342.5 39.9 %block_reduce.1 = f32[192,384]{1,0:T(8,128)} custom-call(f32[2,192,1536]{2,1,0:T(8,128)} %bitcast.10), custom_call_target="tpu_custom_call" | custom-call | tf_op jit(solution)/shard_map/block_reduce/pallas_call | solution.py:432
  382.5 1.6 collective-permute-start.2
  384.1 1.1 negate_select_fusion
  385.2 0.2 constant_dynamic-slice_fusion
  385.4 0.1 collective-permute-start.3
  385.4 1.4 collective-permute-done.3
  386.9 0.0 copy-start.2
  386.9 3.9 fusion.part
  390.8 22.1 %plane_reduce.1 = f32[192,384]{1,0:T(8,128)} custom-call(f32[192,1536]{1,0:T(8,128)} %fusion.part), custom_call_target="tpu_custom_call" | custom-call | tf_op jit(solution)/shard_map/plane_reduce/pallas_call | solution.py:482
  412.9 0.0 collective-permute-done.2
  412.9 0.0 copy-done.2
  412.9 1.8 fusion.13
  414.7 3.3 copy.10
  (5 shorter events, 0.0 us)
Async XLA Ops:
  0.6 5.9 %copy-start.1 = (f32[192,1536]{1,0:T(8,128)S(1)}, f32[192,1536]{1,0:T(8,128)}, u32[]{:S(2)}) copy-start(f32[192,1536]{1,0:T(8,128)} %param.9) | copy-start | bytes 3538948
  3.9 97.9 %collective-permute-start = (f32[192,192]{1,0:T(8,128)S(1)}, f32[192,192]{1,0:T(8,128)S(1)}, u32[]{:S(2)}, u32[]{:S(2)}) collective-permute-start(f32[192,192]{1,0:T(8,128)S(1)} %get-tuple-element.20), channel_id=1, source_target_pairs={{0,0},{1,1},{2,8},{3,9},{4,16},{5,17},{6,24},{7,25},{8,2},{9,3},{1... | collective-permute-start | bytes 442376 | tf_op jit(solution)/shard_map/ppermute | solution.py:815
  4.6 97.2 %collective-permute-start.1 = (f32[192,192]{1,0:T(8,128)S(1)}, f32[192,192]{1,0:T(8,128)S(1)}, u32[]{:S(2)}, u32[]{:S(2)}) collective-permute-start(f32[192,192]{1,0:T(8,128)S(1)} %get-tuple-element.21), channel_id=1, source_target_pairs={{0,1},{1,0},{2,9},{3,8},{4,17},{5,16},{6,25},{7,24},{8,3},{9,2},{1... | collective-permute-start | bytes 442376 | tf_op jit(solution)/shard_map/ppermute | solution.py:815
  69.6 32.2 %copy-start = (f32[192,1536]{1,0:T(8,128)S(1)}, f32[192,1536]{1,0:T(8,128)}, u32[]{:S(2)}) copy-start(f32[192,1536]{1,0:T(8,128)} %and_select_fusion) | copy-start | bytes 3538948
  382.5 30.4 %collective-permute-start.2 = (f32[192,384]{1,0:T(8,128)}, f32[192,384]{1,0:T(8,128)S(1)}, u32[]{:S(2)}, u32[]{:S(2)}) collective-permute-start(f32[192,384]{1,0:T(8,128)} %block_reduce.1), channel_id=1, source_target_pairs={{0,0},{1,1},{2,8},{3,9},{4,16},{5,17},{6,24},{7,25},{8,2},{9,3},{1... | collective-permute-start | bytes 884744 | tf_op jit(solution)/shard_map/ppermute | solution.py:815
  385.4 1.5 collective-permute-start.3
  386.9 26.1 %copy-start.2 = (f32[192,384]{1,0:T(8,128)S(1)}, f32[192,384]{1,0:T(8,128)}, u32[]{:S(2)}) copy-start(f32[192,384]{1,0:T(8,128)} %param.10) | copy-start | bytes 884740
